TPU v7x, 512 devices: a 8x2x16 block of a 8x8x16 slice. The times are simulated.
512 devices in a mesh: grp: 2 (over y), slab: 16 (over z), orb: 8 (over x), rep: 2 (over core).
Axes of the slice: x: 8, y: 2, z: 16, core: 2. Of those that a mesh axis runs over, the one named last changes fastest.
The devices are a block of a 8x8x16 slice.
Arguments:
- orbitals: bfloat16 [256, 32, 1024], P(('grp', 'slab', 'orb')), parts along dimension 0, may hold values from -6 to 6
- corners: int32 [256, 3], P('grp'), parts along dimension 0, may hold values from 0 to 191, as said below
- partners: int32 [256, 24], P(('grp', 'slab', 'orb')), parts along dimension 0, may hold values from -1 to 127, as said below
- kernel: float32 [32, 1024], replicated, may hold values from 0.05 to 5
Outputs:
- exchange_boxes: float32 [256, 32, 1024], P(('grp', 'slab', 'orb')), parts along dimension 0
- exchange_energy: float32 [2], P('grp'), parts along dimension 0
There are 2 independent parts, one for each index of `grp`. A program takes and returns all parts, laid end to end along the dimension named above; an argument that names none is the same for every part. Nothing has to cross between parts.
Inputs may be any that keep to these rules, and one draw needn't show every extreme that they name: corners[i, 2] lies in the slab of orbital i: from 12 * (i // (1 * 8)) to 12 more less one; corners[i, 0] and corners[i, 1] lie below 192. `partners`: row i starts with i itself, names distinct orbitals whose boxes intersect box i (every component of o is above -32 and below 32), and has its -1 entries only after all others.
All inputs are finite; a program needn't handle non-finite values.
Results may differ from a plain program's by a relative error of at most 0.0003.
Values may be sent and summed in bfloat16 or wider, within the bound.
A program may use at most 64 MiB of HBM per device.

v0:
```python
import math

import jax
import jax.numpy as jnp
from jax import lax
from jax.sharding import PartitionSpec as P

G = 192
ZDEV = 12
PB = 4


def joined_along(blocks, dim):
    blocks = jnp.moveaxis(blocks, 0, dim)
    shape = blocks.shape
    return blocks.reshape(*shape[:dim], shape[dim] * shape[dim + 1], *shape[dim + 2 :])


def sent_to_all(array, axis):
    copies = jnp.broadcast_to(array, (lax.axis_size(axis), *array.shape))
    return lax.all_to_all(copies, axis, split_axis=0, concat_axis=0, tiled=True)


def gather_directly(array, axis, dim):
    return joined_along(sent_to_all(array, axis), dim)


def passed_along(array, axis, by):
    size = lax.axis_size(axis)
    return lax.ppermute(array, axis, [(i, (i + by) % size) for i in range(size)])


def over_copies(array, axis):
    everything = sent_to_all(array, axis)
    return jnp.sum(everything, axis=0)


def in_one(arrays, axis):
    ends = [0]
    for a in arrays:
        ends.append(ends[-1] + a.size)
    subtotal = over_copies(jnp.concatenate([a.ravel() for a in arrays]), axis)
    return tuple((subtotal[b:e].reshape(a.shape) for a, b, e in zip(arrays, ends, ends[1:])))


def one_axis_at_a_time(array, axes):
    for axis in axes:
        array = lax.psum(array, axis)
    return array


def wrapped(deltas, lengths):
    halfway = lengths // 2
    return jnp.mod(deltas + halfway, lengths) - halfway


def edge_shifter(offsets, box_edge):
    row_ids = lax.broadcasted_iota(jnp.int32, (offsets.shape[0], box_edge, box_edge), 1)
    col_ids = lax.broadcasted_iota(jnp.int32, (offsets.shape[0], box_edge, box_edge), 2)
    return (col_ids == row_ids + offsets[:, None, None]).astype(jnp.bfloat16)


def plane_shifter(offsets_b, offsets_c, box_edge):
    plane = box_edge * box_edge
    source = lax.broadcasted_iota(jnp.int32, (offsets_b.shape[0], plane, plane), 1)
    target = lax.broadcasted_iota(jnp.int32, (offsets_b.shape[0], plane, plane), 2)
    match_b = source // box_edge == target // box_edge + offsets_b[:, None, None]
    match_c = jnp.mod(source, box_edge) == jnp.mod(target, box_edge) + offsets_c[:, None, None]
    return (match_b & match_c).astype(jnp.bfloat16)


def place_boxes(orbital_boxes, offsets, box_edge):
    stride_along_first = edge_shifter(offsets[:, 0], box_edge)
    displaced_density = jnp.einsum(
        "rkd,rdw->rkw", stride_along_first, orbital_boxes, preferred_element_type=jnp.float32
    ).astype(jnp.bfloat16)
    step_plane = plane_shifter(offsets[:, 1], offsets[:, 2], box_edge)
    return jnp.einsum(
        "pam,pmn->pan", displaced_density, step_plane, preferred_element_type=jnp.float32
    )


def fourier_tables(box_edge):
    grid_ids = jnp.arange(box_edge, dtype=jnp.int32)
    phases = jnp.mod(grid_ids[:, None] * grid_ids[None, :], box_edge)
    angles = phases.astype(jnp.float32) * (2.0 * math.pi / box_edge)
    plane_ids = jnp.arange(box_edge * box_edge, dtype=jnp.int32)
    outer_ids = plane_ids // box_edge
    inner_ids = jnp.mod(plane_ids, box_edge)
    plane_phases = jnp.mod(
        outer_ids[:, None] * outer_ids[None, :] + inner_ids[:, None] * inner_ids[None, :], box_edge
    )
    plane_angles = plane_phases.astype(jnp.float32) * (2.0 * math.pi / box_edge)
    return (jnp.cos(angles), jnp.sin(angles), jnp.cos(plane_angles), jnp.sin(plane_angles))


def edge_rotation(values, matrix):
    return jnp.einsum("ka,pam->pkm", matrix, values, precision=lax.Precision.HIGHEST)


def plane_turn(values, table):
    return jnp.einsum("pam,mn->pan", values, table, precision=lax.Precision.HIGHEST)


def poisson(density, kernel, tables):
    cosine, sine, plane_cos, plane_sin = tables
    plane_real = plane_turn(density, plane_cos)
    plane_imag = -plane_turn(density, plane_sin)
    real_part = edge_rotation(plane_real, cosine) + edge_rotation(plane_imag, sine)
    imag_part = edge_rotation(plane_imag, cosine) - edge_rotation(plane_real, sine)
    real_part = real_part * kernel[None]
    imag_part = imag_part * kernel[None]
    back_real = edge_rotation(real_part, cosine) - edge_rotation(imag_part, sine)
    back_imag = edge_rotation(imag_part, cosine) + edge_rotation(real_part, sine)
    result = plane_turn(back_real, plane_cos) - plane_turn(back_imag, plane_sin)
    box_edge = density.shape[1]
    return result / float(box_edge**3)


def body(orbitals, corners, partners, kernel):
    own_count = orbitals.shape[0]
    box_edge = orbitals.shape[1]
    plane = box_edge * box_edge
    slab_count = lax.axis_size("slab")
    orb_count = lax.axis_size("orb")
    group_size = own_count * orb_count
    slab_position = lax.axis_index("slab")
    halo_depth = (ZDEV + box_edge - 2) // ZDEV
    gathered = gather_directly(orbitals, "orb", 0)
    lower = [gathered]
    upper = [gathered]
    for _ in range(halo_depth):
        lower.append(passed_along(lower[-1], "slab", 1))
        upper.append(passed_along(upper[-1], "slab", -1))
    nearby = jnp.concatenate(lower[::-1] + upper[1:], axis=0)
    rep_count = lax.axis_size("rep")
    rep_index = lax.axis_index("rep")
    half_slots = partners.shape[1] // rep_count
    chosen = lax.dynamic_index_in_dim(
        partners.reshape(own_count, half_slots, rep_count), rep_index, 2, keepdims=False
    )
    first_own = (slab_position * orb_count + lax.axis_index("orb")) * own_count
    owner_ids = jnp.repeat(jnp.arange(own_count, dtype=jnp.int32), half_slots)
    flat_ids = chosen.reshape(own_count * half_slots)
    usable = (flat_ids >= 0).astype(jnp.float32)
    safe_ids = jnp.maximum(flat_ids, 0)
    neighbour_slab = safe_ids // group_size
    slab_step = jnp.mod(neighbour_slab - slab_position + halo_depth, slab_count) - halo_depth
    pool_rows = (slab_step + halo_depth) * group_size + jnp.mod(safe_ids, group_size)
    lengths = jnp.array([G, G, ZDEV * slab_count], jnp.int32)
    own_corners = jnp.take(corners, first_own + owner_ids, axis=0, mode="clip")
    partner_corners = jnp.take(corners, safe_ids, axis=0, mode="clip")
    offsets = wrapped(own_corners - partner_corners, lengths)
    tables = fourier_tables(box_edge)
    block_size = PB
    block_count = own_count * half_slots // block_size

    def block_work(block_index, carry):
        exchange, energy = carry
        first_pair = block_index * block_size
        owner_slot = first_pair // half_slots
        slots = lax.dynamic_slice_in_dim(pool_rows, first_pair, block_size)
        block_offsets = lax.dynamic_slice_in_dim(offsets, first_pair, block_size, 0)
        block_usable = lax.dynamic_slice_in_dim(usable, first_pair, block_size)

        def active(anchor):
            orbital_boxes = jnp.take(nearby, slots, axis=0, mode="clip")
            shifted = (
                place_boxes(orbital_boxes, block_offsets, box_edge) * block_usable[:, None, None]
            )
            centre = lax.dynamic_index_in_dim(orbitals, owner_slot, 0, keepdims=False).astype(
                jnp.float32
            )
            density = centre[None] * shifted
            potential = poisson(density, kernel, tables)
            return (jnp.sum(potential * shifted, axis=0), jnp.sum(density * potential))

        def skipped(anchor):
            return (jnp.zeros((box_edge, plane), jnp.float32), jnp.zeros((), jnp.float32))

        pair_term, energy_part = lax.cond(jnp.sum(block_usable) > 0.0, active, skipped, first_pair)
        previous = lax.dynamic_index_in_dim(exchange, owner_slot, 0, keepdims=False)
        exchange = lax.dynamic_update_index_in_dim(exchange, previous - pair_term, owner_slot, 0)
        return (exchange, energy + energy_part)

    start_state = (jnp.zeros((own_count, box_edge, plane), jnp.float32), jnp.zeros((), jnp.float32))
    exchange, energy = lax.fori_loop(0, block_count, block_work, start_state)
    exchange_total, replica_energy = in_one((exchange, energy), "rep")
    energy_all = one_axis_at_a_time(replica_energy, ("slab", "orb"))
    orbital_total = own_count * slab_count * orb_count
    exchange_energy = -energy_all / (2.0 * orbital_total * box_edge**3)
    return (exchange_total, exchange_energy.reshape(1))


def solution(mesh):
    in_specs = (
        P(("grp", "slab", "orb"), None, None),
        P("grp", None),
        P(("grp", "slab", "orb"), None),
        P(),
    )
    out_specs = (P(("grp", "slab", "orb"), None, None), P("grp"))
    return jax.shard_map(body, mesh=mesh, in_specs=in_specs, out_specs=out_specs, check_vma=False)
```

profile of v0, /device:TPU:80, one launch (start us, length us, event | category | flops | bytes accessed | tf_op | source)
XLA Modules:
  0.0 421.5 jit_solution(8984897013949521450)
XLA Ops:
  0.6 0.9 broadcast_in_dim.47
  1.6 24.8 %all_to_all.11 = bf16[8,1,32,1024]{3,2,1,0:T(8,128)(2,1)S(1)} all-to-all(bf16[8,1,32,1024]{3,2,1,0:T(8,128)(2,1)S(1)} %broadcast_in_dim.47), channel_id=1, replica_groups=mesh['grp'=2,'slab'=16,'orb'=8,'rep'=2] {'orb'}, dimensions={0} | all-to-all | bytes 1048576 | tf_op jit(solution)/shard_map/all_to_all | solution.py:21
  26.4 6.0 %collective-permute-start = (bf16[8,32,1024]{2,1,0:T(8,128)(2,1)S(1)}, bf16[8,32,1024]{2,1,0:T(8,128)(2,1)S(1)}, u32[]{:S(2)}, u32[]{:S(2)}) collective-permute-start(bf16[8,32,1024]{2,1,0:T(8,128)(2,1)S(1)} %bitcast.108), channel_id=1, source_target_pairs={{0,16},{16,32},{32,48},{48,64},{64,80},{80,96},{96,112},{112,128},... | collective-permute-start | bytes 1572872 | tf_op jit(solution)/shard_map/ppermute | solution.py:30
  32.4 39.9 %collective-permute-start.3 = (bf16[8,32,1024]{2,1,0:T(8,128)(2,1)S(1)}, bf16[8,32,1024]{2,1,0:T(8,128)(2,1)S(1)}, u32[]{:S(2)}, u32[]{:S(2)}) collective-permute-start(bf16[8,32,1024]{2,1,0:T(8,128)(2,1)S(1)} %bitcast.109), channel_id=1, source_target_pairs={{0,240},{16,0},{32,16},{48,32},{64,48},{80,64},{96,80},{112,96},{1... | collective-permute-start | bytes 1572872 | tf_op jit(solution)/shard_map/ppermute | solution.py:30
  72.3 8.4 %collective-permute-done = bf16[8,32,1024]{2,1,0:T(8,128)(2,1)S(1)} collective-permute-done((bf16[8,32,1024]{2,1,0:T(8,128)(2,1)S(1)}, bf16[8,32,1024]{2,1,0:T(8,128)(2,1)S(1)}, u32[]{:S(2)}, u32[]{:S(2)}) %collective-permute-start) | collective-permute-done | bytes 524320 | tf_op jit(solution)/shard_map/ppermute | solution.py:30
  80.7 1.9 collective-permute-start.1
  83.3 1.4 reduce.14
  84.7 0.8 copy.19
  86.9 5.2 %collective-permute-start.4 = (bf16[8,32,1024]{2,1,0:T(8,128)(2,1)S(1)}, bf16[8,32,1024]{2,1,0:T(8,128)(2,1)S(1)}, u32[]{:S(2)}, u32[]{:S(2)}) collective-permute-start(bf16[8,32,1024]{2,1,0:T(8,128)(2,1)S(1)} %collective-permute-done.3), channel_id=1, source_target_pairs={{0,240},{16,0},{32,16},{48,32},{64,48},{80,64},{96,80},{112,96},{1... | collective-permute-start | bytes 1572872 | tf_op jit(solution)/shard_map/ppermute | solution.py:30
  92.1 3.3 collective-permute-done.1
  95.4 1.9 collective-permute-start.2
  97.9 3.0 collective-permute-done.4
  100.8 5.6 %collective-permute-start.5 = (bf16[8,32,1024]{2,1,0:T(8,128)(2,1)S(1)}, bf16[8,32,1024]{2,1,0:T(8,128)(2,1)S(1)}, u32[]{:S(2)}, u32[]{:S(2)}) collective-permute-start(bf16[8,32,1024]{2,1,0:T(8,128)(2,1)S(1)} %collective-permute-done.4), channel_id=1, source_target_pairs={{0,240},{16,0},{32,16},{48,32},{64,48},{80,64},{96,80},{112,96},{1... | collective-permute-start | bytes 1572872 | tf_op jit(solution)/shard_map/ppermute | solution.py:30
  106.5 2.7 collective-permute-done.2
  109.5 4.9 %collective-permute-done.5 = bf16[8,32,1024]{2,1,0:T(8,128)(2,1)S(1)} collective-permute-done((bf16[8,32,1024]{2,1,0:T(8,128)(2,1)S(1)}, bf16[8,32,1024]{2,1,0:T(8,128)(2,1)S(1)}, u32[]{:S(2)}, u32[]{:S(2)}) %collective-permute-start.5) | collective-permute-done | bytes 524320 | tf_op jit(solution)/shard_map/ppermute | solution.py:30
  114.4 1.8 copy-done.3
  116.2 254.3 %while.20 = (s32[]{:T(128)}, f32[1,32,1024]{2,1,0:T(8,128)S(1)}, f32[]{:T(128)}, f32[12]{0:T(128)S(1)}, bf16[1,32,1024]{2,1,0:T(8,128)(2,1)S(1)}, /*index=5*/s32...) while((s32[]{:T(128)}, f32[1,32,1024]{2,1,0:T(8,128)S(1)}, ...), condition=%wide.region_6.7_spmd.clone.clone.clone, body=%wide.region_0.6_spmd.clone.clone.clone.sunk | while | flops 7178883072 | bytes 55726804 | solution.py:187
  116.2 0.8 fusion.96
  117.7 3.7 fusion.97
  121.4 79.5 %conditional.5 = (f32[32,1024]{1,0:T(8,128)S(1)}, f32[]{:T(128)}) conditional(s32[]{:T(128)} %convert_element_type.98, () %tuple.99, (bf16[1,32,1024]{2,1,0:T(8,128)(2,1)S(1)}, s32[12,3]{0,1:T(4,128)S(1)}, s32[]{:T(128)}, s32[12]{0:T(128)S(1)}, bf16[56,32,1024]{2,1,0:T(8,128)(2,1)}, /*index=5*/f32[4]{0:T(128)S(1)}, f32[1024,1024]{1,0:T(8,128)}, ...), branch_computations={%region_2.2_spmd, %region_3.5_spmd.clone} | conditional | flops 7162058752 | bytes 51126648 | solution.py:181
  121.5 2.6 gather_fusion
  124.2 4.2 fusion.38
  128.4 17.6 %fusion.31 = f32[4,32,1024]{2,1,0:T(8,128)S(1)} fusion(f32[1024,1024]{1,0:T(8,128)} %get-tuple-element.631, f32[4,32,1024]{2,1,0:T(8,128)S(1)} %fusion.38, f32[32,1024]{1,0:T(8,128)S(1)} %bitcast_convert_fusion), kind=kOutput, calls=%fused_computation.33 | convolution fusion | flops 1610874880 | bytes 5373952 | tf_op jit(solution)/shard_map/while/body/eval_jaxpr/cond/branch_1_fun/pam,mn->pan/dot_general | solution.py:102
  146.0 16.2 %fusion.26 = f32[4,32,1024]{2,1,0:T(8,128)S(1)} fusion(f32[1024,1024]{1,0:T(8,128)S(1)} %copy-done, f32[4,32,1024]{2,1,0:T(8,128)S(1)} %fusion.38, f32[32,1024]{1,0:T(8,128)S(1)} %bitcast_convert_fusion), kind=kOutput, calls=%fused_computation.28 | convolution fusion | flops 1610743808 | bytes 5373952 | tf_op jit(solution)/shard_map/while/body/eval_jaxpr/cond/branch_1_fun/pam,mn->pan/dot_general | solution.py:102
  167.6 16.2 %fusion.25 = f32[4,32,1024]{2,1,0:T(8,128)S(1)} fusion(f32[4,32,1024]{2,1,0:T(8,128)S(1)} %fusion.33, f32[1024,1024]{1,0:T(8,128)S(1)} %copy-done), kind=kOutput, calls=%fused_computation.27 | convolution fusion | flops 1610612736 | bytes 5242880 | tf_op jit(solution)/shard_map/while/body/eval_jaxpr/cond/branch_1_fun/pam,mn->pan/dot_general | solution.py:102
  183.8 16.6 %multiply_reduce_fusion = (f32[]{:T(128)}, f32[32,1024]{1,0:T(8,128)S(1)}) fusion(f32[4,32,1024]{2,1,0:T(8,128)S(1)} %fusion.38, f32[32,1024]{1,0:T(8,128)S(1)} %bitcast_convert_fusion, f32[4,32,1024]{2,1,0:T(8,128)S(1)} %fusion.25, f32[4,32,1024]{2,1,0:T(8,128)S(1)} %fusion.32, f32[1024,1024]{1,0:T(8,128)S(1)} %copy-done), kind=kOutput, calls=%fused_computation.46 | convolution fusion | flops 1611497472 | bytes 6029316 | tf_op jit(solution)/shard_map/while/body/eval_jaxpr/cond/branch_1_fun/pam,mn->pan/dot_general | solution.py:102
  201.0 0.8 fusion.96
  202.4 3.7 fusion.97
  206.1 79.5 %conditional.5 = (f32[32,1024]{1,0:T(8,128)S(1)}, f32[]{:T(128)}) conditional(s32[]{:T(128)} %convert_element_type.98, () %tuple.99, (bf16[1,32,1024]{2,1,0:T(8,128)(2,1)S(1)}, s32[12,3]{0,1:T(4,128)S(1)}, s32[]{:T(128)}, s32[12]{0:T(128)S(1)}, bf16[56,32,1024]{2,1,0:T(8,128)(2,1)}, /*index=5*/f32[4]{0:T(128)S(1)}, f32[1024,1024]{1,0:T(8,128)}, ...), branch_computations={%region_2.2_spmd, %region_3.5_spmd.clone} | conditional | flops 7162058752 | bytes 51126648 | solution.py:181
  206.3 2.6 gather_fusion
  208.9 4.2 fusion.38
  213.2 17.6 %fusion.31 = f32[4,32,1024]{2,1,0:T(8,128)S(1)} fusion(f32[1024,1024]{1,0:T(8,128)} %get-tuple-element.631, f32[4,32,1024]{2,1,0:T(8,128)S(1)} %fusion.38, f32[32,1024]{1,0:T(8,128)S(1)} %bitcast_convert_fusion), kind=kOutput, calls=%fused_computation.33 | convolution fusion | flops 1610874880 | bytes 5373952 | tf_op jit(solution)/shard_map/while/body/eval_jaxpr/cond/branch_1_fun/pam,mn->pan/dot_general | solution.py:102
  230.8 16.2 %fusion.26 = f32[4,32,1024]{2,1,0:T(8,128)S(1)} fusion(f32[1024,1024]{1,0:T(8,128)S(1)} %copy-done, f32[4,32,1024]{2,1,0:T(8,128)S(1)} %fusion.38, f32[32,1024]{1,0:T(8,128)S(1)} %bitcast_convert_fusion), kind=kOutput, calls=%fused_computation.28 | convolution fusion | flops 1610743808 | bytes 5373952 | tf_op jit(solution)/shard_map/while/body/eval_jaxpr/cond/branch_1_fun/pam,mn->pan/dot_general | solution.py:102
  252.4 16.2 %fusion.25 = f32[4,32,1024]{2,1,0:T(8,128)S(1)} fusion(f32[4,32,1024]{2,1,0:T(8,128)S(1)} %fusion.33, f32[1024,1024]{1,0:T(8,128)S(1)} %copy-done), kind=kOutput, calls=%fused_computation.27 | convolution fusion | flops 1610612736 | bytes 5242880 | tf_op jit(solution)/shard_map/while/body/eval_jaxpr/cond/branch_1_fun/pam,mn->pan/dot_general | solution.py:102
  268.5 16.6 %multiply_reduce_fusion = (f32[]{:T(128)}, f32[32,1024]{1,0:T(8,128)S(1)}) fusion(f32[4,32,1024]{2,1,0:T(8,128)S(1)} %fusion.38, f32[32,1024]{1,0:T(8,128)S(1)} %bitcast_convert_fusion, f32[4,32,1024]{2,1,0:T(8,128)S(1)} %fusion.25, f32[4,32,1024]{2,1,0:T(8,128)S(1)} %fusion.32, f32[1024,1024]{1,0:T(8,128)S(1)} %copy-done), kind=kOutput, calls=%fused_computation.46 | convolution fusion | flops 1611497472 | bytes 6029316 | tf_op jit(solution)/shard_map/while/body/eval_jaxpr/cond/branch_1_fun/pam,mn->pan/dot_general | solution.py:102
  285.7 0.8 fusion.96
  287.2 3.7 fusion.97
  290.9 79.5 %conditional.5 = (f32[32,1024]{1,0:T(8,128)S(1)}, f32[]{:T(128)}) conditional(s32[]{:T(128)} %convert_element_type.98, () %tuple.99, (bf16[1,32,1024]{2,1,0:T(8,128)(2,1)S(1)}, s32[12,3]{0,1:T(4,128)S(1)}, s32[]{:T(128)}, s32[12]{0:T(128)S(1)}, bf16[56,32,1024]{2,1,0:T(8,128)(2,1)}, /*index=5*/f32[4]{0:T(128)S(1)}, f32[1024,1024]{1,0:T(8,128)}, ...), branch_computations={%region_2.2_spmd, %region_3.5_spmd.clone} | conditional | flops 7162058752 | bytes 51126648 | solution.py:181
  291.1 2.6 gather_fusion
  293.7 4.2 fusion.38
  297.9 17.6 %fusion.31 = f32[4,32,1024]{2,1,0:T(8,128)S(1)} fusion(f32[1024,1024]{1,0:T(8,128)} %get-tuple-element.631, f32[4,32,1024]{2,1,0:T(8,128)S(1)} %fusion.38, f32[32,1024]{1,0:T(8,128)S(1)} %bitcast_convert_fusion), kind=kOutput, calls=%fused_computation.33 | convolution fusion | flops 1610874880 | bytes 5373952 | tf_op jit(solution)/shard_map/while/body/eval_jaxpr/cond/branch_1_fun/pam,mn->pan/dot_general | solution.py:102
  315.6 16.2 %fusion.26 = f32[4,32,1024]{2,1,0:T(8,128)S(1)} fusion(f32[1024,1024]{1,0:T(8,128)S(1)} %copy-done, f32[4,32,1024]{2,1,0:T(8,128)S(1)} %fusion.38, f32[32,1024]{1,0:T(8,128)S(1)} %bitcast_convert_fusion), kind=kOutput, calls=%fused_computation.28 | convolution fusion | flops 1610743808 | bytes 5373952 | tf_op jit(solution)/shard_map/while/body/eval_jaxpr/cond/branch_1_fun/pam,mn->pan/dot_general | solution.py:102
  337.1 16.2 %fusion.25 = f32[4,32,1024]{2,1,0:T(8,128)S(1)} fusion(f32[4,32,1024]{2,1,0:T(8,128)S(1)} %fusion.33, f32[1024,1024]{1,0:T(8,128)S(1)} %copy-done), kind=kOutput, calls=%fused_computation.27 | convolution fusion | flops 1610612736 | bytes 5242880 | tf_op jit(solution)/shard_map/while/body/eval_jaxpr/cond/branch_1_fun/pam,mn->pan/dot_general | solution.py:102
  353.3 16.6 %multiply_reduce_fusion = (f32[]{:T(128)}, f32[32,1024]{1,0:T(8,128)S(1)}) fusion(f32[4,32,1024]{2,1,0:T(8,128)S(1)} %fusion.38, f32[32,1024]{1,0:T(8,128)S(1)} %bitcast_convert_fusion, f32[4,32,1024]{2,1,0:T(8,128)S(1)} %fusion.25, f32[4,32,1024]{2,1,0:T(8,128)S(1)} %fusion.32, f32[1024,1024]{1,0:T(8,128)S(1)} %copy-done), kind=kOutput, calls=%fused_computation.46 | convolution fusion | flops 1611497472 | bytes 6029316 | tf_op jit(solution)/shard_map/while/body/eval_jaxpr/cond/branch_1_fun/pam,mn->pan/dot_general | solution.py:102
  370.7 4.0 all_to_all.12
  375.5 27.7 %psum.14 = f32[]{:T(128)} all-reduce(f32[]{:T(128)} %bitcast.23), channel_id=1, replica_groups=mesh['grp'=2,'slab'=16,'orb'=8,'rep'=2] {'slab'}, use_global_device_ids=true, to_apply=%region_8.9 | all-reduce | flops 1 | bytes 8 | tf_op jit(solution)/shard_map/psum | solution.py:48
  403.2 15.8 %psum.15 = f32[]{:T(128)} all-reduce(f32[]{:T(128)} %psum.14), channel_id=1, replica_groups=mesh['grp'=2,'slab'=16,'orb'=8,'rep'=2] {'orb'}, use_global_device_ids=true, to_apply=%region_9.10 | all-reduce | flops 1 | bytes 8 | tf_op jit(solution)/shard_map/psum | solution.py:48
  419.7 0.7 reshape.116
  (93 shorter events, 20.5 us)
Async XLA Ops:
  1.5 114.7 %copy-start.1 = (f32[32,1024]{1,0:T(8,128)S(1)}, f32[32,1024]{1,0:T(8,128)}, u32[]{:S(2)}) copy-start(f32[32,1024]{1,0:T(8,128)} %param.12) | copy-start | bytes 393220
  1.5 114.7 %copy-start.2 = (bf16[1,32,1024]{2,1,0:T(8,128)(2,1)S(1)}, bf16[1,32,1024]{2,1,0:T(8,128)(2,1)}, u32[]{:S(2)}) copy-start(bf16[1,32,1024]{2,1,0:T(8,128)(2,1)} %param.9) | copy-start | bytes 196612
  26.4 54.4 %collective-permute-start = (bf16[8,32,1024]{2,1,0:T(8,128)(2,1)S(1)}, bf16[8,32,1024]{2,1,0:T(8,128)(2,1)S(1)}, u32[]{:S(2)}, u32[]{:S(2)}) collective-permute-start(bf16[8,32,1024]{2,1,0:T(8,128)(2,1)S(1)} %bitcast.108), channel_id=1, source_target_pairs={{0,16},{16,32},{32,48},{48,64},{64,80},{80,96},{96,112},{112,128},... | collective-permute-start | bytes 1572872 | tf_op jit(solution)/shard_map/ppermute | solution.py:30
  32.4 54.5 %collective-permute-start.3 = (bf16[8,32,1024]{2,1,0:T(8,128)(2,1)S(1)}, bf16[8,32,1024]{2,1,0:T(8,128)(2,1)S(1)}, u32[]{:S(2)}, u32[]{:S(2)}) collective-permute-start(bf16[8,32,1024]{2,1,0:T(8,128)(2,1)S(1)} %bitcast.109), channel_id=1, source_target_pairs={{0,240},{16,0},{32,16},{48,32},{64,48},{80,64},{96,80},{112,96},{1... | collective-permute-start | bytes 1572872 | tf_op jit(solution)/shard_map/ppermute | solution.py:30
  80.7 14.7 %collective-permute-start.1 = (bf16[8,32,1024]{2,1,0:T(8,128)(2,1)S(1)}, bf16[8,32,1024]{2,1,0:T(8,128)(2,1)S(1)}, u32[]{:S(2)}, u32[]{:S(2)}) collective-permute-start(bf16[8,32,1024]{2,1,0:T(8,128)(2,1)S(1)} %collective-permute-done), channel_id=1, source_target_pairs={{0,16},{16,32},{32,48},{48,64},{64,80},{80,96},{96,112},{112,128},... | collective-permute-start | bytes 1572872 | tf_op jit(solution)/shard_map/ppermute | solution.py:30
  86.9 13.9 %collective-permute-start.4 = (bf16[8,32,1024]{2,1,0:T(8,128)(2,1)S(1)}, bf16[8,32,1024]{2,1,0:T(8,128)(2,1)S(1)}, u32[]{:S(2)}, u32[]{:S(2)}) collective-permute-start(bf16[8,32,1024]{2,1,0:T(8,128)(2,1)S(1)} %collective-permute-done.3), channel_id=1, source_target_pairs={{0,240},{16,0},{32,16},{48,32},{64,48},{80,64},{96,80},{112,96},{1... | collective-permute-start | bytes 1572872 | tf_op jit(solution)/shard_map/ppermute | solution.py:30
  95.4 13.8 %collective-permute-start.2 = (bf16[8,32,1024]{2,1,0:T(8,128)(2,1)S(1)}, bf16[8,32,1024]{2,1,0:T(8,128)(2,1)S(1)}, u32[]{:S(2)}, u32[]{:S(2)}) collective-permute-start(bf16[8,32,1024]{2,1,0:T(8,128)(2,1)S(1)} %collective-permute-done.1), channel_id=1, source_target_pairs={{0,16},{16,32},{32,48},{48,64},{64,80},{80,96},{96,112},{112,128},... | collective-permute-start | bytes 1572872 | tf_op jit(solution)/shard_map/ppermute | solution.py:30
  100.8 13.5 %collective-permute-start.5 = (bf16[8,32,1024]{2,1,0:T(8,128)(2,1)S(1)}, bf16[8,32,1024]{2,1,0:T(8,128)(2,1)S(1)}, u32[]{:S(2)}, u32[]{:S(2)}) collective-permute-start(bf16[8,32,1024]{2,1,0:T(8,128)(2,1)S(1)} %collective-permute-done.4), channel_id=1, source_target_pairs={{0,240},{16,0},{32,16},{48,32},{64,48},{80,64},{96,80},{112,96},{1... | collective-permute-start | bytes 1572872 | tf_op jit(solution)/shard_map/ppermute | solution.py:30
  114.4 1.8 copy-start.3
  128.4 17.6 %copy-start = (f32[1024,1024]{1,0:T(8,128)S(1)}, f32[1024,1024]{1,0:T(8,128)}, u32[]{:S(2)}) copy-start(f32[1024,1024]{1,0:T(8,128)} %get-tuple-element.631) | copy-start | bytes 12582916 | tf_op jit(solution)/shard_map/while/body/eval_jaxpr/cond
  213.1 17.6 %copy-start = (f32[1024,1024]{1,0:T(8,128)S(1)}, f32[1024,1024]{1,0:T(8,128)}, u32[]{:S(2)}) copy-start(f32[1024,1024]{1,0:T(8,128)} %get-tuple-element.631) | copy-start | bytes 12582916 | tf_op jit(solution)/shard_map/while/body/eval_jaxpr/cond
  297.9 17.6 %copy-start = (f32[1024,1024]{1,0:T(8,128)S(1)}, f32[1024,1024]{1,0:T(8,128)}, u32[]{:S(2)}) copy-start(f32[1024,1024]{1,0:T(8,128)} %get-tuple-element.631) | copy-start | bytes 12582916 | tf_op jit(solution)/shard_map/while/body/eval_jaxpr/cond
where the time goes:
time: 424 us; the launch traced here: 422 us
  matrix products  228 us (54%)
  blocking collectives  72.3 us (17%)
  starting transfers between devices  60.6 us (14%)
  waiting for transfers between devices  22.3 us (5%)
  other arithmetic  15.9 us (4%)
  local copies, waits for them, and re-layouts  15.3 us (4%)
  loops' own time  4.28 us (1%)
    dot_general x12, matrix products, plane_turn(): jnp.einsum('pam,mn->pan', values, table, precision=lax.Precision.HIGHEST)  200 us
    ppermute x6, starting transfers between devices, passed_along(): lax.ppermute(array, axis, [(i, (i + by) % size) for i in range(size)])  60.6 us
    psum x2, blocking collectives, one_axis_at_a_time(): array = lax.psum(array, axis)  43.5 us
    all_to_all x2, blocking collectives, sent_to_all(): return lax.all_to_all(copies, axis, split_axis=0, concat_axis=0, tiled=True)  28.8 us
    ppermute x6, waiting for transfers between devices, passed_along(): lax.ppermute(array, axis, [(i, (i + by) % size) for i in range(size)])  22.3 us
    dot_general x24, matrix products, edge_rotation(): jnp.einsum('ka,pam->pkm', matrix, values, precision=lax.Precision.HIGHEST)  15.9 us
    dot_general x3, matrix products, place_boxes(): jnp.einsum('pam,pmn->pan', displaced_density, step_plane, preferred_eleme...  12.6 us
    mul x3, other arithmetic, fourier_tables(): plane_angles = plane_phases.astype(jnp.float32) * (2.0 * math.pi / box_edge)  11 us
  transfers between devices with their start and end apart: 6, of which 5 were waited for; matrix products, arithmetic and copies ran while one was open for 1% of the time, Pallas kernels for 0%

commit v1 on v0

v1 whole, which is shorter than its diff:
```python
import functools, math
import jax, jax.numpy as jnp, numpy as np
from jax import lax
from jax.experimental import pallas as pl
from jax.sharding import PartitionSpec as P
from jax.experimental.pallas import tpu as pltpu

G = 192
ZDEV = 12
B = 32
LANES = 128
PAIRS = 12
GROUPS = 3
MST = 392
F32 = jnp.float32
BF16 = jnp.bfloat16


def plane_tables():
    def th(q, p, bl, a):
        return 2 * np.pi * ((q * bl + p * a) % 32) / 32
    bl = np.repeat(np.arange(8), 32)[:, None]
    a = np.tile(np.arange(32), 8)[:, None]
    lane = np.arange(128)
    g, r = lane // 32, lane % 32
    q = np.where(g > 0, 4 * g, np.where(r < 16, 0, 16))
    p = np.where(g > 0, r, r % 16)
    t = th(q, p, bl, a)
    w0 = np.concatenate([np.cos(t), -np.sin(t)], 1)
    for l in (0, 16):
        w0[:, 128 + l] = np.cos(th(q[l], 16, bl, a))[:, 0]
    t = th(2 + 4 * g, r, bl, a)
    w2 = np.concatenate([np.cos(t), -np.sin(t)], 1)
    l2 = np.arange(256)
    t = th(1 + 4 * (l2 // 32), l2 % 32, bl, a)
    c, s = np.cos(t), np.sin(t)
    w1 = np.block([[c, -s], [s, c]])
    out = []
    for w in (w0, w2, w1):
        w = w.astype(np.float32)
        hi = w.astype(jnp.bfloat16)
        lo = (w - hi.astype(np.float32)).astype(jnp.bfloat16)
        out += [hi, lo]
    return out


def split(x):
    hi = x.astype(BF16)
    return hi, (x - hi.astype(F32)).astype(BF16)


def swap_tile(x):
    t = x.T
    return jnp.concatenate([t[32 * j:32 * j + 32] for j in range(4)], axis=1)


def fft16(re, im, sign):
    def four(a, b, c, d):
        (ar, ai), (br, bi), (cr, ci), (dr, di) = a, b, c, d
        sr, si, tr, ti = ar + cr, ai + ci, ar - cr, ai - ci
        ur, ui, vr, vi = br + dr, bi + di, br - dr, bi - di
        if sign < 0:
            wr, wi = vi, -vr
            return (sr + ur, si + ui), (tr + vi, ti - vr), (sr - ur, si - ui), (tr - vi, ti + vr)
        return (sr + ur, si + ui), (tr - vi, ti + vr), (sr - ur, si - ui), (tr + vi, ti - vr)

    x = list(zip(re, im))
    mid = [four(x[n], x[n + 4], x[n + 8], x[n + 12]) for n in range(4)]
    out = [None] * 16
    h = np.float32(math.sqrt(0.5))
    for k1 in range(4):
        col = []
        for n2 in range(4):
            zr, zi = mid[n2][k1]
            m = n2 * k1
            if m == 0:
                pass
            elif m == 4:
                zr, zi = (zi, -zr) if sign < 0 else (-zi, zr)
            elif m == 2:
                zr, zi = ((zr + zi) * h, (zi - zr) * h) if sign < 0 else ((zr - zi) * h, (zi + zr) * h)
            elif m == 6:
                zr, zi = ((zi - zr) * h, -(zr + zi) * h) if sign < 0 else (-(zr + zi) * h, (zr - zi) * h)
            else:
                c = np.float32(math.cos(2 * math.pi * m / 16))
                s = np.float32(sign * math.sin(2 * math.pi * m / 16))
                zr, zi = zr * c - zi * s, zr * s + zi * c
            col.append((zr, zi))
        res = four(*col)
        for k2 in range(4):
            out[k1 + 4 * k2] = res[k2]
    return [o[0] for o in out], [o[1] for o in out]


def own_tiles(x_ref):
    return [swap_tile(x_ref[0, :, LANES * t:LANES * t + LANES].astype(F32)) for t in range(8)]


def place_centre(tiles, cen):
    for t in range(8):
        for pair in range(4):
            cen[pl.ds(t * 128 + pair, 32, stride=4), :] = tiles[t]


def spectral_kernel(kern_ref, ksp, kdp):
    tiles = [swap_tile(kern_ref[:, LANES * t:LANES * t + LANES]) for t in range(8)]
    whole = jnp.concatenate(tiles, axis=0)

    def exact(a, f):
        one = a.astype(BF16)
        rest = a - one.astype(F32)
        two = rest.astype(BF16)
        three = (rest - two.astype(F32)).astype(BF16)
        return f(one) + (f(two) + f(three))
    row = lax.broadcasted_iota(jnp.int32, (LANES, LANES), 0)
    col = lax.broadcasted_iota(jnp.int32, (LANES, LANES), 1)
    mirror = jnp.bitwise_and(-jnp.bitwise_and(col, 96), 96) + jnp.bitwise_and(-col, 31)
    perm = jnp.where(row == mirror, 1.0, 0.0).astype(BF16)
    row = lax.broadcasted_iota(jnp.int32, (32, 32), 0)
    col = lax.broadcasted_iota(jnp.int32, (32, 32), 1)
    flip = jnp.where(row == jnp.bitwise_and(-col, 31), 1.0, 0.0).astype(BF16)
    lanes = exact(whole, lambda v: jnp.dot(v, perm, preferred_element_type=F32))
    rev = [lanes[32 * t:32 * t + 32] for t in range(8)]
    wide = jnp.concatenate(rev, axis=1)
    wide = exact(wide, lambda v: jnp.dot(flip, v, preferred_element_type=F32))
    rev = [wide[:, LANES * t:LANES * t + LANES] for t in range(8)]
    lane = lax.broadcasted_iota(jnp.int32, (32, LANES), 1)
    sym = []
    for t in range(8):
        other = jnp.where(lane < 32, rev[(8 - t) % 8], rev[7 - t])
        sym.append((tiles[t] + other) * np.float32(0.5))

    def groups(parts):
        out = None
        for g, (t, j) in enumerate(parts):
            v = sym[t]
            if (g - j) % 4:
                v = pltpu.roll(v, 32 * ((g - j) % 4), 1)
            out = v if out is None else jnp.where(lane >= 32 * g, v, out)
        return out
    scale = np.float32(2.0 / 32768)
    u0 = groups([(0, 0), (1, 0), (2, 0), (3, 0)])
    edge = pltpu.roll(sym[4], 16, 1)
    u0 = jnp.where((lane >= 16) & (lane < 32), edge, u0)
    u0 = u0 * scale
    half = np.float32(1.0 / 65536)
    first = sym[0]
    second = pltpu.roll(sym[0], LANES - 16, 1)
    third = sym[4]
    mean0, diff0 = (first + second) * half, (first - second) * half
    fourth = pltpu.roll(sym[4], LANES - 16, 1)
    mean1, diff1 = (third + fourth) * half, (third - fourth) * half
    mean1, diff1 = pltpu.roll(mean1, 16, 1), pltpu.roll(diff1, 16, 1)
    u0 = jnp.where(lane == 0, mean0, jnp.where(lane == 16, mean1, u0))
    d0 = jnp.where(lane == 0, diff0, jnp.where(lane == 16, diff1, jnp.zeros_like(diff0)))
    u1 = groups([(t, 2) for t in range(4)]) * scale
    u2 = groups([(t, 1) for t in range(4)]) * scale
    u3 = groups([(t + 4, 1) for t in range(4)]) * scale
    for pair in range(4):
        for u, v in enumerate((u0, u1, u2, u3)):
            ksp[pl.ds(u * 128 + pair, 16, stride=8), :] = v[:16]
            ksp[pl.ds(u * 128 + 4 + pair, 16, stride=8), :] = v[16:]
        kdp[pl.ds(pair, 16, stride=8), :] = d0[:16]
        kdp[pl.ds(4 + pair, 16, stride=8), :] = d0[16:]


def shift_boxes(pool, tab, zero_block, blocks, m):
    lane = lax.broadcasted_iota(jnp.int32, (8, LANES), 1)
    sub = lax.broadcasted_iota(jnp.int32, (8, LANES), 0)
    a_id = jnp.bitwise_and(lane, 31)
    b_id = sub * 4 + lax.shift_right_logical(lane, 5)

    def one(k, _):
        block, oc, ob, oa, use = tab(k)
        s = ob * 32 + oa
        r = jnp.bitwise_and(s, 127)
        sh = jnp.bitwise_and(lax.shift_right_arithmetic(s, 7), 7)
        lane_by = jnp.bitwise_and(128 - r, 127)
        sub_by = jnp.bitwise_and(8 - sh, 7)
        keep = (a_id + oa >= 0) & (a_id + oa < 32) & (b_id + ob >= 0) & (b_id + ob < 32)
        near = lane < 128 - r
        row = (k // 4) * 128 + k % 4
        for c in range(32):
            src = c + oc
            good = (src >= 0) & (src < 32) & use
            at = jnp.where(good, block + jnp.bitwise_and(src, 1) * blocks, zero_block)
            plane = jnp.where(good, lax.shift_right_arithmetic(src, 1), 0)
            v = pool[at, plane].astype(F32)
            v = pltpu.roll(v, lane_by, 1)
            v = pltpu.roll(v, sub_by, 0)
            w = pltpu.roll(v, 7, 0)
            v = jnp.where(keep, jnp.where(near, v, w), 0.0)
            m[pl.ds(row + 4 * c, 8, stride=MST), :] = v
        return 0
    lax.fori_loop(0, PAIRS, one, 0)


def densities(m, cen, yh, yl):
    def one(i, _):
        row = pl.multiple_of(i * 16, 16)
        crow = pl.multiple_of(jnp.bitwise_and(i, 7) * 16, 16)
        x = [m[pl.ds(pl.multiple_of(MST * t + row, 8), 16), :]
             * cen[pl.ds(pl.multiple_of(128 * t + crow, 16), 16), :] for t in range(8)]
        for h in range(2):
            e, o = x[h] + x[4 + h], x[2 + h] + x[6 + h]
            d, g = x[h] - x[4 + h], x[6 + h] - x[2 + h]
            for at, v in ((0, e + o), (256, e - o), (512, d), (768, g)):
                hi, lo = split(v)
                yh[pl.ds(row, 16), at + LANES * h:at + LANES * h + LANES] = hi
                yl[pl.ds(row, 16), at + LANES * h:at + LANES * h + LANES] = lo
        return 0
    lax.fori_loop(0, 24, one, 0)


CUTS = ((0, 256), (256, 512), (512, 1024))


def turn(yh, yl, w, s, back):
    for (b, e), (wh, wl) in zip(CUTS, w):
        hi, lo = yh[:, b:e], yl[:, b:e]
        dims = (((1,), (1 if back else 0,)), ((), ()))

        def dot(p, q):
            return lax.dot_general(p, q, dims, preferred_element_type=F32)
        out = dot(hi, wh[...]) + dot(lo, wh[...]) + dot(hi, wl[...])
        for t in range(b // LANES, e // LANES):
            s[t] = out[:, t * LANES - b:t * LANES - b + LANES]


def filtered(s, yh, yl, ksp, kdp):
    sub = lax.broadcasted_iota(jnp.int32, (8, LANES), 0)
    lower = sub < 4
    sgn = jnp.where(lower, np.float32(1), np.float32(-1))

    def twiddle(k):
        c = np.float32(math.cos(2 * math.pi * k / 32))
        n = np.float32(math.sin(2 * math.pi * k / 32))
        return jnp.where(lower, np.float32(1), c), jnp.where(lower, np.float32(0), n)

    def job(g, tr, ti, krow, special, energy):
        row = pl.multiple_of(g * 128, 128)
        re = [s[tr, pl.ds(row + 8 * n, 8), :] for n in range(16)]
        im = [s[ti, pl.ds(row + 8 * n, 8), :] for n in range(16)]
        re, im = fft16(re, im, -1)
        zr, zi = [], []
        for k in range(16):
            r, i = re[k], im[k]
            if k:
                c, n = twiddle(k)
                r, i = r * c + i * n, i * c - r * n
            zr.append(pltpu.roll(r, 4, 0) + sgn * r)
            zi.append(pltpu.roll(i, 4, 0) + sgn * i)
        wr, wi = [], []
        for k in range(16):
            km = ksp[pl.ds(krow + 8 * k, 8), :]
            r, i = zr[k] * km, zi[k] * km
            if special:
                kd = kdp[pl.ds(8 * k, 8), :]
                fr, fi = zr[(16 - k) % 16], zi[(16 - k) % 16]
                if k:
                    fr, fi = pltpu.roll(fr, 4, 0), pltpu.roll(fi, 4, 0)
                r, i = r + kd * fr, i - kd * fi
            energy = energy + (r * zr[k] + i * zi[k])
            wr.append(r)
            wi.append(i)
        re, im = [], []
        for k in range(16):
            r = pltpu.roll(wr[k], 4, 0) + sgn * wr[k]
            i = pltpu.roll(wi[k], 4, 0) + sgn * wi[k]
            if k:
                c, n = twiddle(k)
                r, i = r * c - i * n, i * c + r * n
            re.append(r)
            im.append(i)
        re, im = fft16(re, im, 1)
        for n in range(0, 16, 2):
            for t, z in ((tr, re), (ti, im)):
                hi, lo = split(jnp.concatenate([z[n], z[n + 1]], axis=0))
                at = pl.ds(row + 8 * n, 16)
                lanes = pl.ds(pl.multiple_of(t * LANES, LANES), LANES)
                yh[at, lanes] = hi
                yl[at, lanes] = lo
        return energy

    energy = jnp.zeros((8, LANES), F32)

    def first(g, e):
        return job(g, 0, 1, 0, True, e)

    def other(i, e):
        g, u = i // 3, i % 3 + 1
        tr = jnp.where(u == 1, 2, u + 2)
        ti = jnp.where(u == 1, 3, u + 4)
        return job(g, tr, ti, pl.multiple_of(u * 128, 128), False, e)
    energy = lax.fori_loop(0, GROUPS, first, energy)
    return lax.fori_loop(0, 3 * GROUPS, other, energy)


def collect(s, m, acc):
    def one(i, _):
        row = pl.multiple_of(i * 8, 8)
        for h in range(2):
            total = [None] * 4
            for g in range(GROUPS):
                y0, y2, yr, yi = (s[2 * n + h, pl.ds(g * 128 + row, 8), :] for n in range(4))
                p, q = y0 + y2, y0 - y2
                for n, v in enumerate((p + yr, q - yi, p - yr, q + yi)):
                    v = v * m[pl.ds(MST * (2 * n + h) + g * 128 + row, 8), :]
                    total[n] = v if total[n] is None else total[n] + v
            for n in range(4):
                acc[pl.ds((2 * n + h) * 128 + row, 8), :] = total[n]
        return 0
    lax.fori_loop(0, 16, one, 0)


def summed_tiles(acc):
    out = []
    for t in range(8):
        v = [acc[pl.ds(t * 128 + pair, 32, stride=4), :] for pair in range(4)]
        out.append((v[0] + v[1]) + (v[2] + v[3]))
    return out


HALO = 3
KEEP = {0: (0, 16), 1: (0, 16), 2: (0, 10), 3: (0, 4), -1: (0, 16), -2: (6, 10), -3: (12, 4)}
MESH = pl.DeviceIdType.MESH


def sign(v):
    return (v > 0) - (v < 0)


def routes(n_orb):
    out = []
    for core in range(2):
        tree = {}
        for dz in range(-HALO, HALO + 1):
            for dx in range(1 - n_orb // 2, n_orb // 2 + 1):
                if (dz, dx) == (0, 0):
                    continue
                way = sign(dx)
                if dx == n_orb // 2 and core == 1 and dz in (0, -1, -2):
                    way = -1
                if core == 0:
                    tree[dz, dx] = (sign(dz), 0) if dz else (0, way)
                else:
                    tree[dz, dx] = (0, way) if dx else (sign(dz), 0)
        out.append(tree)
    return out


def schedule(tree, core):
    def steps(p):
        dz, dx = p
        return (abs(dz) + abs(dx), abs(dx) if core == 0 else abs(dz), p)
    return sorted(tree, key=steps)


def kernel_body(n_slab, n_orb, x_ref, corners, partners, kern_hbm, *rest):
    w_hbm, rest = rest[:6], rest[6:]
    out_ref, en_ref = rest[:2]
    (pool, m, yh, yl, s, ksp, kdp, cen, acc, kern, part, other, echip, ex, ez) = rest[2:17]
    w_ref = rest[17:23]
    local_sem, send_sem, recv_sem, swap_send, swap_recv, tail_sem, ready_one, ready_two = rest[23:]
    here_x = lax.axis_index("orb")
    here_z = lax.axis_index("slab")
    rep = lax.axis_index("rep")
    blocks = (2 * HALO + 1) * n_orb
    zero_block = 2 * blocks

    loads = [pltpu.make_async_copy(kern_hbm, kern, local_sem.at[0])]
    loads += [pltpu.make_async_copy(a, b, local_sem.at[1 + i]) for i, (a, b) in enumerate(zip(w_hbm, w_ref))]
    for load in loads:
        load.start()

    def at_slab(step):
        return {"slab": lax.rem(here_z + step + n_slab, n_slab)}

    def at_orb(step):
        return {"orb": lax.rem(here_x + step + n_orb, n_orb)}
    sibling = {"rep": 1 - rep}

    barrier = pltpu.get_barrier_semaphore()
    for peer in (at_orb(1), at_orb(-1), at_slab(1), at_slab(-1), sibling):
        pl.semaphore_signal(barrier, inc=1, device_id=peer, device_id_type=MESH)

    tiles = own_tiles(x_ref)
    for t in range(8):
        acc[pl.ds(t, 32, stride=8), :] = tiles[t]
    own_block = HALO * n_orb + here_x
    mine = rep * blocks + own_block
    for c in range(16):
        even = acc[16 * c:16 * c + 8, :]
        odd = acc[16 * c + 8:16 * c + 16, :]
        pool[mine, c] = jnp.where(rep == 0, even, odd).astype(BF16)
    pool[zero_block, 0] = jnp.zeros((8, LANES), BF16)
    pl.semaphore_wait(barrier, 5)

    def slot(core, p):
        first, count = KEEP[p[0]]
        block = core * blocks + (p[0] + HALO) * n_orb + lax.rem(here_x + p[1] + n_orb, n_orb)
        return pool.at[block, pl.ds(first, count)]

    def index(p):
        return (p[0] + HALO) * n_orb + (p[1] + n_orb) % n_orb

    def swap(core, p):
        return pltpu.make_async_remote_copy(
            src_ref=slot(core, p), dst_ref=slot(core, p), send_sem=swap_send.at[index(p)],
            recv_sem=swap_recv.at[index(p)], device_id=sibling, device_id_type=MESH)

    def pass_on(core, p, hop):
        first, count = KEEP[p[0]]
        held = (p[0] - hop[0], p[1] - hop[1])
        x_slot = lax.rem(here_x + held[1] + n_orb, n_orb)
        src = pool.at[core * blocks + (held[0] + HALO) * n_orb + x_slot, pl.ds(first, count)]
        dst = pool.at[core * blocks + (p[0] + HALO) * n_orb + x_slot, pl.ds(first, count)]
        peer = at_slab(-hop[0]) if hop[0] else at_orb(-hop[1])
        return pltpu.make_async_remote_copy(
            src_ref=src, dst_ref=dst, send_sem=send_sem.at[index(p)], recv_sem=recv_sem.at[index(p)],
            device_id=peer, device_id_type=MESH)

    def arrival(core, p):
        return pltpu.make_async_remote_copy(
            src_ref=slot(core, p), dst_ref=slot(core, p), send_sem=send_sem.at[index(p)],
            recv_sem=recv_sem.at[index(p)], device_id=sibling, device_id_type=MESH)

    trees = routes(n_orb)

    def spread(core, held):
        for p, hop in trees[core].items():
            h = (p[0] - hop[0], p[1] - hop[1])
            if h == held or (h[0] == held[0] and (h[1] - held[1]) % n_orb == 0):
                pass_on(core, p, hop).start()
        swap(core, held).start()

    for core in range(2):
        @pl.when(rep == core)
        def _(core=core):
            spread(core, (0, 0))

    place_centre(tiles, cen)
    loads[0].wait()
    spectral_kernel(kern, ksp, kdp)

    for core in range(2):
        @pl.when(rep == core)
        def _(core=core):
            for p in schedule(trees[core], core):
                arrival(core, p).wait_recv()
                spread(core, p)
            for p in trees[core]:
                arrival(core, p).wait_send()
            for p in [(0, 0)] + list(trees[core]):
                swap(core, p).wait_send()
                swap(1 - core, p).wait_recv()

    def signal_far(sem):
        for step in (HALO, -HALO):
            pl.semaphore_signal(sem, inc=1, device_id=at_slab(step), device_id_type=MESH)
    signal_far(ready_one)

    own = here_z * n_orb + here_x

    def wrap(v):
        v = v + G // 2
        v = jnp.where(v < 0, v + G, jnp.where(v >= G, v - G, v))
        return v - G // 2

    def tab(k):
        j = partners[0, 2 * k + rep]
        use = j >= 0
        j = jnp.where(use, j, own)
        o = [wrap(corners[own, d] - corners[j, d]) for d in range(3)]
        dz = lax.div(j, n_orb) - here_z
        dz = jnp.where(dz > n_slab // 2, dz - n_slab, jnp.where(dz < -(n_slab // 2), dz + n_slab, dz))
        dz = jnp.clip(dz, -HALO, HALO)
        return (dz + HALO) * n_orb + lax.rem(j, n_orb), o[2], o[1], o[0], use

    shift_boxes(pool, tab, zero_block, blocks, m)
    densities(m, cen, yh, yl)
    for load in loads[1:]:
        load.wait()
    w = ((w_ref[0], w_ref[1]), (w_ref[2], w_ref[3]), (w_ref[4], w_ref[5]))
    pl.semaphore_wait(ready_one, 2)
    signal_far(ready_two)
    turn(yh, yl, w, s, False)
    energy = filtered(s, yh, yl, ksp, kdp)
    pl.semaphore_wait(ready_two, 2)

    echip[0] = jnp.sum(energy, axis=0, keepdims=True)
    swap_energy = pltpu.make_async_remote_copy(
        src_ref=echip.at[0], dst_ref=echip.at[1], send_sem=tail_sem.at[0], recv_sem=tail_sem.at[1],
        device_id=sibling, device_id_type=MESH)
    swap_energy.start()
    turn(yh, yl, w, s, True)
    swap_energy.wait()
    ex[here_x] = echip[0] + echip[1]

    def to_all(buf, here, size, at, sems):
        copies = []
        for step in range(1, size):
            copies.append(pltpu.make_async_remote_copy(
                src_ref=buf.at[here], dst_ref=buf.at[here], send_sem=sems[0].at[sems[1] + step],
                recv_sem=sems[0].at[sems[1] + size + step], device_id=at(step), device_id_type=MESH))
        return copies

    def from_all(buf, here, size, at, sems):
        for step in range(1, size):
            there = lax.rem(here - step + size, size)
            pltpu.make_async_remote_copy(
                src_ref=buf.at[there], dst_ref=buf.at[there], send_sem=sems[0].at[sems[1] + step],
                recv_sem=sems[0].at[sems[1] + size + step], device_id=at(step), device_id_type=MESH).wait_recv()
    x_sems = (tail_sem, 4)
    z_sems = (tail_sem, 4 + 2 * n_orb)
    x_copies = to_all(ex, here_x, n_orb, at_orb, x_sems)
    for copy in x_copies:
        copy.start()
    collect(s, m, acc)
    res = summed_tiles(acc)
    for t in range(8):
        part[t] = res[t]
    swap_part = pltpu.make_async_remote_copy(
        src_ref=part, dst_ref=other, send_sem=tail_sem.at[2], recv_sem=tail_sem.at[3],
        device_id=sibling, device_id_type=MESH)
    swap_part.start()
    from_all(ex, here_x, n_orb, at_orb, x_sems)
    ez[here_z] = functools.reduce(lambda a, b: a + b, [ex[i] for i in range(n_orb)])
    z_copies = to_all(ez, here_z, n_slab, at_slab, z_sems)
    for copy in z_copies:
        copy.start()
    swap_part.wait()
    for t in range(8):
        out_ref[0, :, LANES * t:LANES * t + LANES] = -swap_tile(part[t] + other[t])
    for copy in x_copies:
        copy.wait_send()
    from_all(ez, here_z, n_slab, at_slab, z_sems)
    total = functools.reduce(lambda a, b: a + b, [ez[i] for i in range(n_slab)])
    for copy in z_copies:
        copy.wait_send()
    en_ref[0] = jnp.sum(total) * np.float32(-1.0 / (2.0 * n_slab * n_orb * B ** 3))


def body(n_slab, n_orb, orbitals, corners, partners, kernel):
    blocks = (2 * HALO + 1) * n_orb
    vmem = pl.BlockSpec(memory_space=pltpu.VMEM)
    smem = pl.BlockSpec(memory_space=pltpu.SMEM)
    hbm = pl.BlockSpec(memory_space=pl.ANY)
    dma = pltpu.SemaphoreType.DMA
    weights = [jnp.asarray(w) for w in plane_tables()]
    return pl.pallas_call(
        functools.partial(kernel_body, n_slab, n_orb),
        out_shape=(jax.ShapeDtypeStruct((1, B, B * B), F32), jax.ShapeDtypeStruct((1,), F32)),
        in_specs=[vmem, smem, smem, hbm] + [hbm] * 6,
        out_specs=(vmem, smem),
        scratch_shapes=[
            pltpu.VMEM((2 * blocks + 1, 16, 8, LANES), BF16),
            pltpu.VMEM((8 * MST, LANES), F32),
            pltpu.VMEM((384, 1024), BF16),
            pltpu.VMEM((384, 1024), BF16),
            pltpu.VMEM((8, 384, LANES), F32),
            pltpu.VMEM((512, LANES), F32),
            pltpu.VMEM((128, LANES), F32),
            pltpu.VMEM((1024, LANES), F32),
            pltpu.VMEM((1024, LANES), F32),
            pltpu.VMEM((B, B * B), F32),
            pltpu.VMEM((8, B, LANES), F32),
            pltpu.VMEM((8, B, LANES), F32),
            pltpu.VMEM((2, 1, LANES), F32),
            pltpu.VMEM((n_orb, 1, LANES), F32),
            pltpu.VMEM((n_slab, 1, LANES), F32),
            *[pltpu.VMEM(w.shape, BF16) for w in weights],
            dma((7,)),
            dma((blocks,)),
            dma((blocks,)),
            dma((blocks,)),
            dma((blocks,)),
            dma((4 + 2 * n_orb + 2 * n_slab,)),
            pltpu.SemaphoreType.REGULAR,
            pltpu.SemaphoreType.REGULAR,
        ],
        compiler_params=pltpu.CompilerParams(
            collective_id=0, has_side_effects=True, vmem_limit_bytes=48 * 2**20),
    )(orbitals, corners, partners, kernel, *weights)


def solution(mesh):
    in_specs = (
        P(("grp", "slab", "orb"), None, None),
        P("grp", None),
        P(("grp", "slab", "orb"), None),
        P(),
    )
    out_specs = (P(("grp", "slab", "orb"), None, None), P("grp"))
    step = functools.partial(body, mesh.shape["slab"], mesh.shape["orb"])
    return jax.shard_map(step, mesh=mesh, in_specs=in_specs, out_specs=out_specs, check_vma=False)
```

time: 424 us -> 106 us (0.25)
  matrix products: 228 us -> 0 us
  Pallas kernels: 0 us -> 95.3 us
  blocking collectives: 72.3 us -> 0 us
  starting transfers between devices: 60.6 us -> 0 us
  waiting for transfers between devices: 22.3 us -> 0 us
  other arithmetic: 15.9 us -> 0 us
  local copies, waits for them, and re-layouts: 15.3 us -> 8.09 us
  loops' own time: 4.28 us -> 0 us
    dot_general x39 -> x0, matrix products: 228 us -> none  [the longest x12 200 us: plane_turn(): jnp.einsum('pam,mn->pan', values, table, precision=lax.Precision.HIGHEST)]
    pallas_call x0 -> x1, Pallas kernels: none -> 95.3 us  [body(): pl.pallas_call(functools.partial(kernel_body, n_slab, n_orb), out_shape=(...]
    ppermute x6 -> x0, starting transfers between devices: 60.6 us -> none  [passed_along(): lax.ppermute(array, axis, [(i, (i + by) % size) for i in range(size)])]
    psum x2 -> x0, blocking collectives: 43.5 us -> none  [one_axis_at_a_time(): array = lax.psum(array, axis)]
    all_to_all x2 -> x0, blocking collectives: 28.8 us -> none  [sent_to_all(): return lax.all_to_all(copies, axis, split_axis=0, concat_axis=0, tiled=True)]
    ppermute x6 -> x0, waiting for transfers between devices: 22.3 us -> none  [passed_along(): lax.ppermute(array, axis, [(i, (i + by) % size) for i in range(size)])]
    mul x9 -> x0, other arithmetic: 11.1 us -> none  [the longest x3 11 us: fourier_tables(): plane_angles = plane_phases.astype(jnp.float32) * (2.0 * math.pi / box_edge)]
    gather x5 -> x0, local copies, waits for them, and re-layouts: 8.92 us -> none  [the longest x3 7.8 us: active(): orbital_boxes = jnp.take(nearby, slots, axis=0, mode='clip')]
  transfers between devices with their start and end apart: 6 -> 0, of which waited for: 5 -> 0; matrix products, arithmetic and copies ran while one was open for 1% -> 0% of each run, Pallas kernels for 0% -> 0%
where the time goes in v1:
time: 106 us
  Pallas kernels  95.3 us (90%)
  local copies, waits for them, and re-layouts  8.09 us (8%)
  between operations  2.43 us (2%)
    pallas_call x1, Pallas kernels, body(): pl.pallas_call(functools.partial(kernel_body, n_slab, n_orb), out_shape=(...  95.3 us
    unnamed x20, local copies, waits for them, and re-layouts  8.09 us

profile of v1, /device:TPU:80, one launch (start us, length us, event | category | flops | bytes accessed | tf_op | source)
XLA Modules:
  0.0 105.8 jit_solution(13962903383280141670)
XLA Ops:
  0.6 0.0 copy-start.8
  0.6 0.0 copy-start.7
  0.6 0.8 copy.12.corners
  1.5 0.0 copy-done.8
  1.5 0.0 copy-done.7
  1.5 0.0 copy-start
  1.5 1.0 copy-done
  2.5 0.0 copy-start.1
  2.5 1.0 copy-done.1
  3.6 0.0 copy-start.2
  3.6 0.9 copy-done.2
  4.5 0.0 copy-start.3
  4.5 0.9 copy-done.3
  5.4 0.0 copy-start.4
  5.4 0.9 copy-done.4
  6.3 0.0 copy-start.5
  6.3 0.9 copy-done.5
  7.2 0.0 copy-start.6
  7.2 0.9 copy-done.6
  8.1 95.3 %shard_map.113 = (f32[1,32,1024]{2,1,0:T(8,128)S(1)}, f32[1]{0:T(128)}) custom-call(bf16[1,32,1024]{2,1,0:T(8,128)(2,1)S(1)} %copy-done.7, s32[128,3]{1,0:T(8,128)S(1)} %copy.12.corners, s32[1,24]{1,0:T(1,128)S(1)} %copy-done.8, f32[32,1024]{1,0:T(8,128)S(1)} %copy-done.2, bf16[256,256]{1,0:T(8,128)(2,1)S(1)} %copy-done.6, bf16[256,256]{1,0:T(8,128)(2,1)S(1)} %copy-done.5, ...), custom_call_target="tpu_custom_call" | custom-call | tf_op jit(solution)/shard_map/pallas_call | solution.py:551
  103.4 0.7 copy.15
Async XLA Ops:
  0.6 0.8 copy-start.8
  0.6 0.8 copy-start.7
  1.5 1.0 copy-start
  2.5 1.0 copy-start.1
  3.6 0.9 copy-start.2
  4.5 0.9 copy-start.3
  5.4 0.9 copy-start.4
  6.3 0.9 copy-start.5
  7.2 0.9 copy-start.6

commit v2 on v1

--- a/solution.py
+++ b/solution.py
@@ -580,7 +580,7 @@
             pltpu.SemaphoreType.REGULAR,
         ],
         compiler_params=pltpu.CompilerParams(
-            collective_id=0, has_side_effects=True, vmem_limit_bytes=48 * 2**20),
+            collective_id=0, has_side_effects=True, vmem_limit_bytes=67043328),
     )(orbitals, corners, partners, kernel, *weights)
 
 

time: 106 us -> 100 us (0.943)
  local copies, waits for them, and re-layouts: 8.09 us -> 2.99 us
    unnamed x20 -> x2, local copies, waits for them, and re-layouts: 8.09 us -> 2.99 us
where the time goes in v2:
time: 100 us
  Pallas kernels  94.7 us (95%)
  local copies, waits for them, and re-layouts  2.99 us (3%)
  between operations  2.45 us (2%)
    pallas_call x1, Pallas kernels, body(): pl.pallas_call(functools.partial(kernel_body, n_slab, n_orb), out_shape=(...  94.7 us
    unnamed x2, local copies, waits for them, and re-layouts  2.99 us

profile of v2, /device:TPU:80, one launch (start us, length us, event | category | flops | bytes accessed | tf_op | source)
XLA Modules:
  0.0 100.1 jit_solution(11098557946421343051)
XLA Ops:
  0.6 1.4 %copy.12.corners = s32[128,3]{1,0:T(8,128)} copy(s32[128,3]{0,1:T(4,128)} %param.11) | data formatting | bytes 3072 | tf_op args[1]
  2.0 94.7 %shard_map.113 = (f32[1,32,1024]{2,1,0:T(8,128)}, f32[1]{0:T(128)}) custom-call(bf16[1,32,1024]{2,1,0:T(8,128)(2,1)} %x_ref.1, s32[128,3]{1,0:T(8,128)} %copy.12.corners, s32[1,24]{1,0:T(1,128)} %partners.1, f32[32,1024]{1,0:T(8,128)} %kern_hbm.1, bf16[256,256]{1,0:T(8,128)(2,1)} %constant.12.clone.rest_0_, bf16[256,256]{1,0:T(8,128)(2,1)} %constant.13.clone.rest_1_, ...), custom_call_target="tpu_custom_call" | custom-call | tf_op jit(solution)/shard_map/pallas_call | solution.py:551
  96.7 1.6 %copy.15 = f32[1,32,1024]{2,1,0:T(8,128)} copy(f32[1,32,1024]{2,1,0:T(8,128)} %get-tuple-element.4) | data formatting | bytes 262144

commit v3 on v2

--- a/solution.py
+++ b/solution.py
@@ -322,12 +322,20 @@
 
 
 HALO = 3
-KEEP = {0: (0, 16), 1: (0, 16), 2: (0, 10), 3: (0, 4), -1: (0, 16), -2: (6, 10), -3: (12, 4)}
+KEEP = (
+    {0: (0, 16), 1: (0, 16), 2: (0, 10), 3: (0, 4), -1: (1, 15), -2: (7, 9), -3: (13, 3)},
+    {0: (0, 16), 1: (0, 15), 2: (0, 9), 3: (0, 3), -1: (0, 16), -2: (6, 10), -3: (12, 4)},
+)
 MESH = pl.DeviceIdType.MESH
 
 
 def sign(v):
     return (v > 0) - (v < 0)
+
+
+ORB_HOP = {1: 1, 2: 2, 3: 3, 4: 4}
+SLAB_HOP = {1: 1, 2: 2, 3: 3}
+LATE_HOP = {1: 1, 2: 1, 3: 1, 4: 1}
 
 
 def routes(n_orb):
@@ -342,37 +350,37 @@
                 if dx == n_orb // 2 and core == 1 and dz in (0, -1, -2):
                     way = -1
                 if core == 0:
-                    tree[dz, dx] = (sign(dz), 0) if dz else (0, way)
+                    tree[dz, dx] = (sign(dz) * SLAB_HOP[abs(dz)], 0) if dz else (0, way * ORB_HOP[abs(dx)])
                 else:
-                    tree[dz, dx] = (0, way) if dx else (sign(dz), 0)
+                    tree[dz, dx] = (0, way * LATE_HOP[abs(dx)]) if dx else (sign(dz) * SLAB_HOP[abs(dz)], 0)
         out.append(tree)
     return out
 
 
-def schedule(tree, core):
-    def steps(p):
-        dz, dx = p
-        return (abs(dz) + abs(dx), abs(dx) if core == 0 else abs(dz), p)
-    return sorted(tree, key=steps)
-
-
-def kernel_body(n_slab, n_orb, x_ref, corners, partners, kern_hbm, *rest):
+def held_as(tree, p, n_orb):
+    dz, dx = p[0] - tree[p][0], p[1] - tree[p][1]
+    return dz, (dx + n_orb // 2 - 1) % n_orb - n_orb // 2 + 1
+
+
+def schedule(tree, n_orb):
+    def depth(p):
+        return 0 if p == (0, 0) else 1 + depth(held_as(tree, p, n_orb))
+    return sorted(tree, key=lambda p: (depth(p), abs(p[0]) + abs(p[1]), p))
+
+
+def kernel_body(n_slab, n_orb, x_hbm, corners_hbm, partners_hbm, kern_hbm, *rest):
     w_hbm, rest = rest[:6], rest[6:]
     out_ref, en_ref = rest[:2]
-    (pool, m, yh, yl, s, ksp, kdp, cen, acc, kern, part, other, echip, ex, ez) = rest[2:17]
-    w_ref = rest[17:23]
-    local_sem, send_sem, recv_sem, swap_send, swap_recv, tail_sem, ready_one, ready_two = rest[23:]
+    (pool, m, yh, yl, s, ksp, kdp, cen, acc, kern, part, other, ex, ez) = rest[2:16]
+    w_ref = rest[16:22]
+    x_ref, corners, partners = rest[22:25]
+    local_sem, send_sem, recv_sem, swap_send, swap_recv, tail_sem, ready_one, ready_two = rest[25:]
     here_x = lax.axis_index("orb")
     here_z = lax.axis_index("slab")
     rep = lax.axis_index("rep")
     blocks = (2 * HALO + 1) * n_orb
     zero_block = 2 * blocks
 
-    loads = [pltpu.make_async_copy(kern_hbm, kern, local_sem.at[0])]
-    loads += [pltpu.make_async_copy(a, b, local_sem.at[1 + i]) for i, (a, b) in enumerate(zip(w_hbm, w_ref))]
-    for load in loads:
-        load.start()
-
     def at_slab(step):
         return {"slab": lax.rem(here_z + step + n_slab, n_slab)}
 
@@ -380,10 +388,25 @@
         return {"orb": lax.rem(here_x + step + n_orb, n_orb)}
     sibling = {"rep": 1 - rep}
 
+    trees = routes(n_orb)
+
+    def at(hop):
+        return {**at_slab(hop[0]), **at_orb(hop[1])}
     barrier = pltpu.get_barrier_semaphore()
-    for peer in (at_orb(1), at_orb(-1), at_slab(1), at_slab(-1), sibling):
-        pl.semaphore_signal(barrier, inc=1, device_id=peer, device_id_type=MESH)
-
+    pl.semaphore_signal(barrier, inc=1, device_id=sibling, device_id_type=MESH)
+    for core in range(2):
+        @pl.when(rep == core)
+        def _(core=core):
+            for hop in sorted(set(trees[core].values())):
+                pl.semaphore_signal(barrier, inc=1, device_id=at(hop), device_id_type=MESH)
+
+    x_load = pltpu.make_async_copy(x_hbm, x_ref, local_sem.at[0])
+    x_load.start()
+    loads = [pltpu.make_async_copy(a, b, local_sem.at[1 + i]) for i, (a, b) in enumerate(zip(
+        (kern_hbm, corners_hbm, partners_hbm) + w_hbm, (kern, corners, partners) + w_ref))]
+    for load in loads:
+        load.start()
+    x_load.wait()
     tiles = own_tiles(x_ref)
     for t in range(8):
         acc[pl.ds(t, 32, stride=8), :] = tiles[t]
@@ -394,10 +417,17 @@
         odd = acc[16 * c + 8:16 * c + 16, :]
         pool[mine, c] = jnp.where(rep == 0, even, odd).astype(BF16)
     pool[zero_block, 0] = jnp.zeros((8, LANES), BF16)
-    pl.semaphore_wait(barrier, 5)
+    for core in range(2):
+        @pl.when(rep == core)
+        def _(core=core):
+            pl.semaphore_wait(barrier, len(set(trees[core].values())) + 1)
+
+    def signal_far(sem):
+        for step in (HALO, -HALO):
+            pl.semaphore_signal(sem, inc=1, device_id=at_slab(step), device_id_type=MESH)
 
     def slot(core, p):
-        first, count = KEEP[p[0]]
+        first, count = KEEP[core][p[0]]
         block = core * blocks + (p[0] + HALO) * n_orb + lax.rem(here_x + p[1] + n_orb, n_orb)
         return pool.at[block, pl.ds(first, count)]
 
@@ -410,12 +440,12 @@
             recv_sem=swap_recv.at[index(p)], device_id=sibling, device_id_type=MESH)
 
     def pass_on(core, p, hop):
-        first, count = KEEP[p[0]]
+        first, count = KEEP[core][p[0]]
         held = (p[0] - hop[0], p[1] - hop[1])
         x_slot = lax.rem(here_x + held[1] + n_orb, n_orb)
         src = pool.at[core * blocks + (held[0] + HALO) * n_orb + x_slot, pl.ds(first, count)]
         dst = pool.at[core * blocks + (p[0] + HALO) * n_orb + x_slot, pl.ds(first, count)]
-        peer = at_slab(-hop[0]) if hop[0] else at_orb(-hop[1])
+        peer = at((-hop[0], -hop[1]))
         return pltpu.make_async_remote_copy(
             src_ref=src, dst_ref=dst, send_sem=send_sem.at[index(p)], recv_sem=recv_sem.at[index(p)],
             device_id=peer, device_id_type=MESH)
@@ -425,13 +455,11 @@
             src_ref=slot(core, p), dst_ref=slot(core, p), send_sem=send_sem.at[index(p)],
             recv_sem=recv_sem.at[index(p)], device_id=sibling, device_id_type=MESH)
 
-    trees = routes(n_orb)
-
     def spread(core, held):
-        for p, hop in trees[core].items():
-            h = (p[0] - hop[0], p[1] - hop[1])
-            if h == held or (h[0] == held[0] and (h[1] - held[1]) % n_orb == 0):
-                pass_on(core, p, hop).start()
+        tree = trees[core]
+        for p in sorted(tree, key=lambda p: -abs(tree[p][0]) - abs(tree[p][1])):
+            if held_as(tree, p, n_orb) == held:
+                pass_on(core, p, tree[p]).start()
         swap(core, held).start()
 
     for core in range(2):
@@ -439,6 +467,7 @@
         def _(core=core):
             spread(core, (0, 0))
 
+    signal_far(ready_one)
     place_centre(tiles, cen)
     loads[0].wait()
     spectral_kernel(kern, ksp, kdp)
@@ -446,7 +475,7 @@
     for core in range(2):
         @pl.when(rep == core)
         def _(core=core):
-            for p in schedule(trees[core], core):
+            for p in schedule(trees[core], n_orb):
                 arrival(core, p).wait_recv()
                 spread(core, p)
             for p in trees[core]:
@@ -455,10 +484,8 @@
                 swap(core, p).wait_send()
                 swap(1 - core, p).wait_recv()
 
-    def signal_far(sem):
-        for step in (HALO, -HALO):
-            pl.semaphore_signal(sem, inc=1, device_id=at_slab(step), device_id_type=MESH)
-    signal_far(ready_one)
+    pl.semaphore_wait(ready_one, 2)
+    signal_far(ready_two)
 
     own = here_z * n_orb + here_x
 
@@ -466,6 +493,9 @@
         v = v + G // 2
         v = jnp.where(v < 0, v + G, jnp.where(v >= G, v - G, v))
         return v - G // 2
+
+    loads[1].wait()
+    loads[2].wait()
 
     def tab(k):
         j = partners[0, 2 * k + rep]
@@ -479,65 +509,60 @@
 
     shift_boxes(pool, tab, zero_block, blocks, m)
     densities(m, cen, yh, yl)
-    for load in loads[1:]:
+    for load in loads[3:]:
         load.wait()
     w = ((w_ref[0], w_ref[1]), (w_ref[2], w_ref[3]), (w_ref[4], w_ref[5]))
-    pl.semaphore_wait(ready_one, 2)
-    signal_far(ready_two)
     turn(yh, yl, w, s, False)
     energy = filtered(s, yh, yl, ksp, kdp)
     pl.semaphore_wait(ready_two, 2)
 
-    echip[0] = jnp.sum(energy, axis=0, keepdims=True)
-    swap_energy = pltpu.make_async_remote_copy(
-        src_ref=echip.at[0], dst_ref=echip.at[1], send_sem=tail_sem.at[0], recv_sem=tail_sem.at[1],
-        device_id=sibling, device_id_type=MESH)
-    swap_energy.start()
+    me = 2 * here_x + rep
+    ex[me] = jnp.sum(energy, axis=0, keepdims=True)
+
+    def to_slab(step, cross, back):
+        other_rep = 1 - rep if cross else rep
+        there = 2 * lax.rem(here_x - step + n_orb, n_orb) + other_rep
+        cell = ex.at[there if back else me]
+        n = 2 * step + cross
+        return pltpu.make_async_remote_copy(
+            src_ref=cell, dst_ref=cell, send_sem=tail_sem.at[2 + n], recv_sem=tail_sem.at[2 + 2 * n_orb + n],
+            device_id={**at_orb(step), "rep": other_rep}, device_id_type=MESH)
+
+    def to_column(step, back):
+        cell = ez.at[lax.rem(here_z - step + n_slab, n_slab) if back else here_z]
+        first = 2 + 4 * n_orb
+        return pltpu.make_async_remote_copy(
+            src_ref=cell, dst_ref=cell, send_sem=tail_sem.at[first + step],
+            recv_sem=tail_sem.at[first + n_slab + step], device_id=at_slab(step), device_id_type=MESH)
+    near = [(step, cross) for step in range(n_orb) for cross in range(2) if step or cross]
+    near.sort(key=lambda v: -min(v[0], n_orb - v[0]))
+    far = sorted(range(1, n_slab), key=lambda v: -min(v, n_slab - v))
+    for step, cross in near:
+        to_slab(step, cross, False).start()
     turn(yh, yl, w, s, True)
-    swap_energy.wait()
-    ex[here_x] = echip[0] + echip[1]
-
-    def to_all(buf, here, size, at, sems):
-        copies = []
-        for step in range(1, size):
-            copies.append(pltpu.make_async_remote_copy(
-                src_ref=buf.at[here], dst_ref=buf.at[here], send_sem=sems[0].at[sems[1] + step],
-                recv_sem=sems[0].at[sems[1] + size + step], device_id=at(step), device_id_type=MESH))
-        return copies
-
-    def from_all(buf, here, size, at, sems):
-        for step in range(1, size):
-            there = lax.rem(here - step + size, size)
-            pltpu.make_async_remote_copy(
-                src_ref=buf.at[there], dst_ref=buf.at[there], send_sem=sems[0].at[sems[1] + step],
-                recv_sem=sems[0].at[sems[1] + size + step], device_id=at(step), device_id_type=MESH).wait_recv()
-    x_sems = (tail_sem, 4)
-    z_sems = (tail_sem, 4 + 2 * n_orb)
-    x_copies = to_all(ex, here_x, n_orb, at_orb, x_sems)
-    for copy in x_copies:
-        copy.start()
     collect(s, m, acc)
     res = summed_tiles(acc)
     for t in range(8):
         part[t] = res[t]
     swap_part = pltpu.make_async_remote_copy(
-        src_ref=part, dst_ref=other, send_sem=tail_sem.at[2], recv_sem=tail_sem.at[3],
+        src_ref=part, dst_ref=other, send_sem=tail_sem.at[0], recv_sem=tail_sem.at[1],
         device_id=sibling, device_id_type=MESH)
     swap_part.start()
-    from_all(ex, here_x, n_orb, at_orb, x_sems)
-    ez[here_z] = functools.reduce(lambda a, b: a + b, [ex[i] for i in range(n_orb)])
-    z_copies = to_all(ez, here_z, n_slab, at_slab, z_sems)
-    for copy in z_copies:
-        copy.start()
+    for step, cross in near:
+        to_slab(step, cross, True).wait_recv()
+    ez[here_z] = functools.reduce(lambda a, b: a + b, [ex[i] for i in range(2 * n_orb)])
+    for step in far:
+        to_column(step, False).start()
     swap_part.wait()
     for t in range(8):
         out_ref[0, :, LANES * t:LANES * t + LANES] = -swap_tile(part[t] + other[t])
-    for copy in x_copies:
-        copy.wait_send()
-    from_all(ez, here_z, n_slab, at_slab, z_sems)
+    for step, cross in near:
+        to_slab(step, cross, False).wait_send()
+    for step in far:
+        to_column(step, True).wait_recv()
     total = functools.reduce(lambda a, b: a + b, [ez[i] for i in range(n_slab)])
-    for copy in z_copies:
-        copy.wait_send()
+    for step in far:
+        to_column(step, False).wait_send()
     en_ref[0] = jnp.sum(total) * np.float32(-1.0 / (2.0 * n_slab * n_orb * B ** 3))
 
 
@@ -551,7 +576,7 @@
     return pl.pallas_call(
         functools.partial(kernel_body, n_slab, n_orb),
         out_shape=(jax.ShapeDtypeStruct((1, B, B * B), F32), jax.ShapeDtypeStruct((1,), F32)),
-        in_specs=[vmem, smem, smem, hbm] + [hbm] * 6,
+        in_specs=[hbm] * 10,
         out_specs=(vmem, smem),
         scratch_shapes=[
             pltpu.VMEM((2 * blocks + 1, 16, 8, LANES), BF16),
@@ -566,16 +591,18 @@
             pltpu.VMEM((B, B * B), F32),
             pltpu.VMEM((8, B, LANES), F32),
             pltpu.VMEM((8, B, LANES), F32),
-            pltpu.VMEM((2, 1, LANES), F32),
-            pltpu.VMEM((n_orb, 1, LANES), F32),
+            pltpu.VMEM((2 * n_orb, 1, LANES), F32),
             pltpu.VMEM((n_slab, 1, LANES), F32),
             *[pltpu.VMEM(w.shape, BF16) for w in weights],
-            dma((7,)),
+            pltpu.VMEM((1, B, B * B), BF16),
+            pltpu.SMEM(corners.shape, jnp.int32),
+            pltpu.SMEM(partners.shape, jnp.int32),
+            dma((10,)),
             dma((blocks,)),
             dma((blocks,)),
             dma((blocks,)),
             dma((blocks,)),
-            dma((4 + 2 * n_orb + 2 * n_slab,)),
+            dma((2 + 4 * n_orb + 2 * n_slab,)),
             pltpu.SemaphoreType.REGULAR,
             pltpu.SemaphoreType.REGULAR,
         ],

time: 100 us -> 89.7 us (0.90)
  Pallas kernels: 94.7 us -> 84.1 us
    pallas_call x1, Pallas kernels: 94.7 us -> 84.1 us  [body(): pl.pallas_call(functools.partial(kernel_body, n_slab, n_orb), out_shape=(...]
where the time goes in v3:
time: 89.7 us; the launch traced here: 89.5 us
  Pallas kernels  84.1 us (94%)
  local copies, waits for them, and re-layouts  2.99 us (3%)
  between operations  2.45 us (3%)
    pallas_call x1, Pallas kernels, body(): pl.pallas_call(functools.partial(kernel_body, n_slab, n_orb), out_shape=(...  84.1 us
    unnamed x2, local copies, waits for them, and re-layouts  2.99 us

profile of v3, /device:TPU:80, one launch (start us, length us, event | category | flops | bytes accessed | tf_op | source)
XLA Modules:
  0.0 89.5 jit_solution(1738693097163182674)
XLA Ops:
  0.6 1.4 %copy.12.corners_hbm = s32[128,3]{1,0:T(8,128)} copy(s32[128,3]{0,1:T(4,128)} %param.11) | data formatting | bytes 3072 | tf_op args[1]
  2.0 84.1 %shard_map.113 = (f32[1,32,1024]{2,1,0:T(8,128)}, f32[1]{0:T(128)}) custom-call(bf16[1,32,1024]{2,1,0:T(8,128)(2,1)} %x_hbm.1, s32[128,3]{1,0:T(8,128)} %copy.12.corners_hbm, s32[1,24]{1,0:T(1,128)} %partners_hbm.1, f32[32,1024]{1,0:T(8,128)} %kern_hbm.1, bf16[256,256]{1,0:T(8,128)(2,1)} %constant.12.clone.rest_0_, bf16[256,256]{1,0:T(8,128)(2,1)} %constant.13.clone.rest_1_, ...), custom_call_target="tpu_custom_call" | custom-call | tf_op jit(solution)/shard_map/pallas_call | solution.py:576
  86.1 1.6 %copy.15 = f32[1,32,1024]{2,1,0:T(8,128)} copy(f32[1,32,1024]{2,1,0:T(8,128)} %get-tuple-element.4) | data formatting | bytes 262144

commit v4 on v3

--- a/solution.py
+++ b/solution.py
@@ -164,14 +164,14 @@
         kdp[pl.ds(4 + pair, 16, stride=8), :] = d0[16:]
 
 
-def shift_boxes(pool, tab, zero_block, blocks, m):
+def shift_boxes(pool, tab, zero_plane, half_planes, m):
     lane = lax.broadcasted_iota(jnp.int32, (8, LANES), 1)
     sub = lax.broadcasted_iota(jnp.int32, (8, LANES), 0)
     a_id = jnp.bitwise_and(lane, 31)
     b_id = sub * 4 + lax.shift_right_logical(lane, 5)
 
     def one(k, _):
-        block, oc, ob, oa, use = tab(k)
+        base, oc, ob, oa, use = tab(k)
         s = ob * 32 + oa
         r = jnp.bitwise_and(s, 127)
         sh = jnp.bitwise_and(lax.shift_right_arithmetic(s, 7), 7)
@@ -180,17 +180,19 @@
         keep = (a_id + oa >= 0) & (a_id + oa < 32) & (b_id + ob >= 0) & (b_id + ob < 32)
         near = lane < 128 - r
         row = (k // 4) * 128 + k % 4
-        for c in range(32):
-            src = c + oc
-            good = (src >= 0) & (src < 32) & use
-            at = jnp.where(good, block + jnp.bitwise_and(src, 1) * blocks, zero_block)
-            plane = jnp.where(good, lax.shift_right_arithmetic(src, 1), 0)
-            v = pool[at, plane].astype(F32)
-            v = pltpu.roll(v, lane_by, 1)
-            v = pltpu.roll(v, sub_by, 0)
-            w = pltpu.roll(v, 7, 0)
-            v = jnp.where(keep, jnp.where(near, v, w), 0.0)
-            m[pl.ds(row + 4 * c, 8, stride=MST), :] = v
+        odd = jnp.bitwise_and(oc, 1)
+        for par in range(2):
+            first = base + jnp.where(odd == par, 0, 1) * half_planes
+            off = jnp.where(use, lax.shift_right_arithmetic(oc + par, 1), 64)
+            for n in range(16):
+                at = n + off
+                good = (at >= 0) & (at < 16)
+                v = pool[jnp.where(good, first + at, zero_plane)].astype(F32)
+                v = pltpu.roll(v, lane_by, 1)
+                v = pltpu.roll(v, sub_by, 0)
+                w = pltpu.roll(v, 7, 0)
+                v = jnp.where(keep, jnp.where(near, v, w), 0.0)
+                m[pl.ds(row + 4 * (2 * n + par), 8, stride=MST), :] = v
         return 0
     lax.fori_loop(0, PAIRS, one, 0)
 
@@ -369,17 +371,17 @@
 
 
 def kernel_body(n_slab, n_orb, x_hbm, corners_hbm, partners_hbm, kern_hbm, *rest):
-    w_hbm, rest = rest[:6], rest[6:]
+    w_hbm, rest = rest[:2], rest[2:]
     out_ref, en_ref = rest[:2]
     (pool, m, yh, yl, s, ksp, kdp, cen, acc, kern, part, other, ex, ez) = rest[2:16]
-    w_ref = rest[16:22]
-    x_ref, corners, partners = rest[22:25]
-    local_sem, send_sem, recv_sem, swap_send, swap_recv, tail_sem, ready_one, ready_two = rest[25:]
+    w_ref = rest[16:18]
+    x_ref, corners, partners = rest[18:21]
+    local_sem, send_sem, recv_sem, swap_send, swap_recv, tail_sem, ready_one, ready_two = rest[21:]
     here_x = lax.axis_index("orb")
     here_z = lax.axis_index("slab")
     rep = lax.axis_index("rep")
     blocks = (2 * HALO + 1) * n_orb
-    zero_block = 2 * blocks
+    zero_plane = 2 * blocks * 16
 
     def at_slab(step):
         return {"slab": lax.rem(here_z + step + n_slab, n_slab)}
@@ -415,8 +417,8 @@
     for c in range(16):
         even = acc[16 * c:16 * c + 8, :]
         odd = acc[16 * c + 8:16 * c + 16, :]
-        pool[mine, c] = jnp.where(rep == 0, even, odd).astype(BF16)
-    pool[zero_block, 0] = jnp.zeros((8, LANES), BF16)
+        pool[mine * 16 + c] = jnp.where(rep == 0, even, odd).astype(BF16)
+    pool[zero_plane] = jnp.zeros((8, LANES), BF16)
     for core in range(2):
         @pl.when(rep == core)
         def _(core=core):
@@ -429,7 +431,7 @@
     def slot(core, p):
         first, count = KEEP[core][p[0]]
         block = core * blocks + (p[0] + HALO) * n_orb + lax.rem(here_x + p[1] + n_orb, n_orb)
-        return pool.at[block, pl.ds(first, count)]
+        return pool.at[pl.ds(block * 16 + first, count)]
 
     def index(p):
         return (p[0] + HALO) * n_orb + (p[1] + n_orb) % n_orb
@@ -443,8 +445,8 @@
         first, count = KEEP[core][p[0]]
         held = (p[0] - hop[0], p[1] - hop[1])
         x_slot = lax.rem(here_x + held[1] + n_orb, n_orb)
-        src = pool.at[core * blocks + (held[0] + HALO) * n_orb + x_slot, pl.ds(first, count)]
-        dst = pool.at[core * blocks + (p[0] + HALO) * n_orb + x_slot, pl.ds(first, count)]
+        src = pool.at[pl.ds((core * blocks + (held[0] + HALO) * n_orb + x_slot) * 16 + first, count)]
+        dst = pool.at[pl.ds((core * blocks + (p[0] + HALO) * n_orb + x_slot) * 16 + first, count)]
         peer = at((-hop[0], -hop[1]))
         return pltpu.make_async_remote_copy(
             src_ref=src, dst_ref=dst, send_sem=send_sem.at[index(p)], recv_sem=recv_sem.at[index(p)],
@@ -501,17 +503,18 @@
         j = partners[0, 2 * k + rep]
         use = j >= 0
         j = jnp.where(use, j, own)
-        o = [wrap(corners[own, d] - corners[j, d]) for d in range(3)]
+        o = [wrap(corners[d, own] - corners[d, j]) for d in range(3)]
         dz = lax.div(j, n_orb) - here_z
         dz = jnp.where(dz > n_slab // 2, dz - n_slab, jnp.where(dz < -(n_slab // 2), dz + n_slab, dz))
         dz = jnp.clip(dz, -HALO, HALO)
-        return (dz + HALO) * n_orb + lax.rem(j, n_orb), o[2], o[1], o[0], use
-
-    shift_boxes(pool, tab, zero_block, blocks, m)
+        return ((dz + HALO) * n_orb + lax.rem(j, n_orb)) * 16, o[2], o[1], o[0], use
+
+    shift_boxes(pool, tab, zero_plane, blocks * 16, m)
     densities(m, cen, yh, yl)
     for load in loads[3:]:
         load.wait()
-    w = ((w_ref[0], w_ref[1]), (w_ref[2], w_ref[3]), (w_ref[4], w_ref[5]))
+    w = [(w_ref[0].at[pl.ds(a, 256)], w_ref[0].at[pl.ds(a + 256, 256)]) for a in (0, 512)]
+    w.append((w_ref[1].at[pl.ds(0, 512)], w_ref[1].at[pl.ds(512, 512)]))
     turn(yh, yl, w, s, False)
     energy = filtered(s, yh, yl, ksp, kdp)
     pl.semaphore_wait(ready_two, 2)
@@ -555,7 +558,9 @@
         to_column(step, False).start()
     swap_part.wait()
     for t in range(8):
-        out_ref[0, :, LANES * t:LANES * t + LANES] = -swap_tile(part[t] + other[t])
+        kern[:, LANES * t:LANES * t + LANES] = -swap_tile(part[t] + other[t])
+    flush = pltpu.make_async_copy(kern, out_ref.at[0], local_sem.at[0])
+    flush.start()
     for step, cross in near:
         to_slab(step, cross, False).wait_send()
     for step in far:
@@ -563,23 +568,24 @@
     total = functools.reduce(lambda a, b: a + b, [ez[i] for i in range(n_slab)])
     for step in far:
         to_column(step, False).wait_send()
+    flush.wait()
     en_ref[0] = jnp.sum(total) * np.float32(-1.0 / (2.0 * n_slab * n_orb * B ** 3))
 
 
 def body(n_slab, n_orb, orbitals, corners, partners, kernel):
     blocks = (2 * HALO + 1) * n_orb
-    vmem = pl.BlockSpec(memory_space=pltpu.VMEM)
     smem = pl.BlockSpec(memory_space=pltpu.SMEM)
     hbm = pl.BlockSpec(memory_space=pl.ANY)
     dma = pltpu.SemaphoreType.DMA
-    weights = [jnp.asarray(w) for w in plane_tables()]
+    tables = plane_tables()
+    weights = [jnp.asarray(np.concatenate(tables[:4])), jnp.asarray(np.concatenate(tables[4:]))]
     return pl.pallas_call(
         functools.partial(kernel_body, n_slab, n_orb),
         out_shape=(jax.ShapeDtypeStruct((1, B, B * B), F32), jax.ShapeDtypeStruct((1,), F32)),
-        in_specs=[hbm] * 10,
-        out_specs=(vmem, smem),
+        in_specs=[hbm] * 6,
+        out_specs=(hbm, smem),
         scratch_shapes=[
-            pltpu.VMEM((2 * blocks + 1, 16, 8, LANES), BF16),
+            pltpu.VMEM((2 * blocks * 16 + 1, 8, LANES), BF16),
             pltpu.VMEM((8 * MST, LANES), F32),
             pltpu.VMEM((384, 1024), BF16),
             pltpu.VMEM((384, 1024), BF16),
@@ -595,9 +601,9 @@
             pltpu.VMEM((n_slab, 1, LANES), F32),
             *[pltpu.VMEM(w.shape, BF16) for w in weights],
             pltpu.VMEM((1, B, B * B), BF16),
-            pltpu.SMEM(corners.shape, jnp.int32),
+            pltpu.SMEM(corners.shape[::-1], jnp.int32),
             pltpu.SMEM(partners.shape, jnp.int32),
-            dma((10,)),
+            dma((6,)),
             dma((blocks,)),
             dma((blocks,)),
             dma((blocks,)),
@@ -608,7 +614,7 @@
         ],
         compiler_params=pltpu.CompilerParams(
             collective_id=0, has_side_effects=True, vmem_limit_bytes=67043328),
-    )(orbitals, corners, partners, kernel, *weights)
+    )(orbitals, corners.T, partners, kernel, *weights)
 
 
 def solution(mesh):

time: 89.7 us -> 87.4 us (0.974)
  local copies, waits for them, and re-layouts: 2.99 us -> 1.57 us
    unnamed x2 -> x1, local copies, waits for them, and re-layouts: 2.99 us -> 1.57 us
where the time goes in v4:
time: 87.4 us; the launch traced here: 87.3 us
  Pallas kernels  83.3 us (95%)
  between operations  2.45 us (3%)
  local copies, waits for them, and re-layouts  1.57 us (2%)
    pallas_call x1, Pallas kernels, body(): pl.pallas_call(functools.partial(kernel_body, n_slab, n_orb), out_shape=(...  83.3 us

profile of v4, /device:TPU:80, one launch (start us, length us, event | category | flops | bytes accessed | tf_op | source)
XLA Modules:
  0.0 87.3 jit_solution(15656991698460175134)
XLA Ops:
  0.6 83.3 %shard_map.77 = (f32[1,32,1024]{2,1,0:T(8,128)}, f32[1]{0:T(128)}) custom-call(bf16[1,32,1024]{2,1,0:T(8,128)(2,1)} %x_hbm.1, s32[3,128]{1,0:T(4,128)} %bitcast.1, s32[1,24]{1,0:T(1,128)} %partners_hbm.1, f32[32,1024]{1,0:T(8,128)} %kern_hbm.1, bf16[1024,256]{1,0:T(8,128)(2,1)} %constant.4.clone.rest_0_, bf16[1024,512]{1,0:T(8,128)(2,1)} %constant.5.clone.rest_1_), custom_call_target="tpu_custom_call" | custom-call | tf_op jit(solution)/shard_map/pallas_call | solution.py:582
  83.9 1.6 %copy.10 = f32[1,32,1024]{2,1,0:T(8,128)} copy(f32[1,32,1024]{2,1,0:T(8,128)} %get-tuple-element.4) | data formatting | bytes 262144

commit v5 on v4

--- a/solution.py
+++ b/solution.py
@@ -337,7 +337,7 @@
 
 ORB_HOP = {1: 1, 2: 2, 3: 3, 4: 4}
 SLAB_HOP = {1: 1, 2: 2, 3: 3}
-LATE_HOP = {1: 1, 2: 1, 3: 1, 4: 1}
+LATE_HOP = {1: 1, 2: 2, 3: 1, 4: 2}
 
 
 def routes(n_orb):
@@ -349,9 +349,9 @@
                 if (dz, dx) == (0, 0):
                     continue
                 way = sign(dx)
-                if dx == n_orb // 2 and core == 1 and dz in (0, -1, -2):
+                if dx == n_orb // 2 and core == 0 and dz in (0, -1, -2):
                     way = -1
-                if core == 0:
+                if core == 1:
                     tree[dz, dx] = (sign(dz) * SLAB_HOP[abs(dz)], 0) if dz else (0, way * ORB_HOP[abs(dx)])
                 else:
                     tree[dz, dx] = (0, way * LATE_HOP[abs(dx)]) if dx else (sign(dz) * SLAB_HOP[abs(dz)], 0)
@@ -459,7 +459,7 @@
 
     def spread(core, held):
         tree = trees[core]
-        for p in sorted(tree, key=lambda p: -abs(tree[p][0]) - abs(tree[p][1])):
+        for p in sorted(tree, key=lambda p: abs(tree[p][0]) + abs(tree[p][1])):
             if held_as(tree, p, n_orb) == held:
                 pass_on(core, p, tree[p]).start()
         swap(core, held).start()

time: 87.4 us -> 84.2 us (0.963)
  Pallas kernels: 83.3 us -> 80 us
    pallas_call x1, Pallas kernels: 83.3 us -> 80 us  [body(): pl.pallas_call(functools.partial(kernel_body, n_slab, n_orb), out_shape=(...]
where the time goes in v5:
time: 84.2 us; the launch traced here: 84 us
  Pallas kernels  80 us (95%)
  between operations  2.45 us (3%)
  local copies, waits for them, and re-layouts  1.57 us (2%)
    pallas_call x1, Pallas kernels, body(): pl.pallas_call(functools.partial(kernel_body, n_slab, n_orb), out_shape=(...  80 us

profile of v5, /device:TPU:80, one launch (start us, length us, event | category | flops | bytes accessed | tf_op | source)
XLA Modules:
  0.0 84.0 jit_solution(13904896358046995965)
XLA Ops:
  0.6 80.0 %shard_map.77 = (f32[1,32,1024]{2,1,0:T(8,128)}, f32[1]{0:T(128)}) custom-call(bf16[1,32,1024]{2,1,0:T(8,128)(2,1)} %x_hbm.1, s32[3,128]{1,0:T(4,128)} %bitcast.1, s32[1,24]{1,0:T(1,128)} %partners_hbm.1, f32[32,1024]{1,0:T(8,128)} %kern_hbm.1, bf16[1024,256]{1,0:T(8,128)(2,1)} %constant.4.clone.rest_0_, bf16[1024,512]{1,0:T(8,128)(2,1)} %constant.5.clone.rest_1_), custom_call_target="tpu_custom_call" | custom-call | tf_op jit(solution)/shard_map/pallas_call | solution.py:582
  80.7 1.6 %copy.10 = f32[1,32,1024]{2,1,0:T(8,128)} copy(f32[1,32,1024]{2,1,0:T(8,128)} %get-tuple-element.4) | data formatting | bytes 262144
